TPU v7x, 256 devices: a whole 4x4x8 slice. The times are simulated.
256 devices in a mesh: row: 8 (over y, z_lo), col: 32 (over x, z_hi, core).
Axes of the slice: x: 4, y: 4, z: 8 (z_hi: 4, z_lo: 2; z = z_hi * 2 + z_lo), core: 2. Of those that a mesh axis runs over, the one named last changes fastest.
Arguments:
- queries: bfloat16 [32768, 128], P(('row', 'col')), may hold values from -8 to 8
- key_rows: bfloat16 [32768, 128], P(('row', 'col')), may hold values from -8 to 8
- value_rows: bfloat16 [32768, 128], P(('row', 'col')), may hold values from -6 to 6
- grad_output: bfloat16 [32768, 128], P(('row', 'col')), may hold values from -6 to 6
- positions: int32 [32768], replicated, may hold values from 0 to 32767, as said below
Outputs:
- grad_queries: bfloat16 [32768, 128], P(('row', 'col'))
- grad_keys: bfloat16 [32768, 128], P(('row', 'col'))
- grad_values: bfloat16 [32768, 128], P(('row', 'col'))
Inputs may be any that keep to these rules, and one draw needn't show every extreme that they name: `positions`: a permutation: each of 0 to 32767 appears once.
All inputs are finite; a program needn't handle non-finite values.
Results may differ from a plain program's by a relative error of at most 0.0068.
Values may be sent and summed in bfloat16 or wider, within the bound.
A program may use at most 128 MiB of HBM per device.

v0:
```python
import math

import jax
import jax.numpy as jnp
from jax import lax
from jax.sharding import PartitionSpec as P


def side_by_side(arrays, axis, dim, along):
    both = jnp.concatenate(arrays, axis=along)
    out, at, outs = (lax.all_gather(both, axis, axis=dim, tiled=True), 0, [])
    for a in arrays:
        outs.append(lax.slice_in_dim(out, at, at + a.shape[along], axis=along))
        at += a.shape[along]
    return tuple(outs)


def sent_to_all(array, axis):
    devices = lax.axis_size(axis)
    return lax.all_to_all(
        jnp.broadcast_to(array[None], (devices, *array.shape)), axis, 0, 0, tiled=True
    )


def all_in_one(array, axis):
    leaves = jax.tree.leaves(array)
    sequence = sorted(range(len(leaves)), key=lambda k: -leaves[k].size)
    width = (1, *leaves[sequence[0]].shape)[-1]
    lines = [
        jnp.pad(leaves[k].reshape(-1), (0, -leaves[k].size % width)).reshape(-1, width)
        for k in sequence
    ]
    both, at, found = (sent_to_all(jnp.concatenate(lines), axis), 0, {})
    for k, line in zip(sequence, lines):
        section = both[:, at : at + len(line)].reshape(len(both), -1)
        found[k] = section[:, : leaves[k].size].reshape(-1, *leaves[k].shape)
        at += len(line)
    numbers = iter(range(len(leaves)))
    return jax.tree.map(lambda _: found[next(numbers)], array)


def joined_by_halves(pieces, combine):
    while len(jax.tree.leaves(pieces)[0]) > 1:
        pieces = jax.vmap(combine)(
            *(jax.tree.map(lambda part: part[side::2], pieces) for side in (0, 1))
        )
    return jax.tree.map(lambda part: part[0], pieces)


def combined_all(array, axis, combine):
    pieces = all_in_one(array, axis)
    return joined_by_halves(pieces, combine)


def cut_along(array, dim, devices):
    before, after = (array.shape[:dim], array.shape[dim + 1 :])
    return jnp.moveaxis(array.reshape(*before, devices, -1, *after), dim, 0)


def summed_on_arrival(array, axis, dim):
    devices = lax.axis_size(axis)
    tiles = lax.all_to_all(cut_along(array, dim, devices), axis, 0, 0, tiled=True)
    return jnp.sum(tiles, axis=0)


def in_one_piece(arrays, axis, dim, along):
    widths = [a.shape[along] for a in arrays]
    both = jnp.concatenate(arrays, axis=along)
    out = summed_on_arrival(both, axis, dim)
    return tuple(jnp.split(out, [sum(widths[:k]) for k in range(1, len(widths))], axis=along))


def combine_stats(left, right):
    new_max = jnp.maximum(left[0], right[0])
    left_scale = jnp.exp(left[0] - new_max)
    right_scale = jnp.exp(right[0] - new_max)
    return (
        new_max,
        left[1] * left_scale + right[1] * right_scale,
        left[2] * left_scale + right[2] * right_scale,
    )


def block_products(queries_all, grads_all, key_block, value_block, score_scale):
    scores = (
        jnp.einsum("qd,kd->qk", queries_all, key_block, preferred_element_type=jnp.float32)
        * score_scale
    )
    dprobs = jnp.einsum("qd,kd->qk", grads_all, value_block, preferred_element_type=jnp.float32)
    return (scores, dprobs)


def local_stats(queries_all, grads_all, keys_all, values_all, query_order, key_order, score_scale):
    key_count = keys_all.shape[0]
    block_rows = 512
    query_count = queries_all.shape[0]

    def local_advance(state, which):
        run_max, run_sum, run_dot = state
        begin_row = which * block_rows
        key_block = lax.dynamic_slice_in_dim(keys_all, begin_row, block_rows, 0)
        value_block = lax.dynamic_slice_in_dim(values_all, begin_row, block_rows, 0)
        order_block = lax.dynamic_slice_in_dim(key_order, begin_row, block_rows, 0)
        scores, dprobs = block_products(queries_all, grads_all, key_block, value_block, score_scale)
        allowed = query_order[:, None] >= order_block[None, :]
        new_max = jnp.maximum(run_max, jnp.max(jnp.where(allowed, scores, -1e30), axis=1))
        weights = jnp.where(allowed, jnp.exp(scores - new_max[:, None]), 0.0)
        rescale = jnp.exp(run_max - new_max)
        run_sum = run_sum * rescale + jnp.sum(weights, axis=1)
        run_dot = run_dot * rescale + jnp.sum(weights * dprobs, axis=1)
        saved = None
        return ((new_max, run_sum, run_dot), saved)

    initial = (
        jnp.full((query_count,), -1e30, jnp.float32),
        jnp.zeros((query_count,), jnp.float32),
        jnp.zeros((query_count,), jnp.float32),
    )
    result, saved = lax.scan(
        local_advance, initial, jnp.arange(key_count // block_rows, dtype=jnp.int32)
    )
    return (result, saved)


def tile_gradients(
    queries_all,
    grads_all,
    keys_all,
    values_all,
    query_order,
    key_order,
    log_total,
    delta,
    score_scale,
):
    key_count = keys_all.shape[0]
    block_rows = 512
    width = queries_all.shape[1]

    def tile_advance(grad_query, item):
        which = item[0]
        begin_row = which * block_rows
        key_block = lax.dynamic_slice_in_dim(keys_all, begin_row, block_rows, 0)
        value_block = lax.dynamic_slice_in_dim(values_all, begin_row, block_rows, 0)
        order_block = lax.dynamic_slice_in_dim(key_order, begin_row, block_rows, 0)
        scores, dprobs = block_products(queries_all, grads_all, key_block, value_block, score_scale)
        allowed = query_order[:, None] >= order_block[None, :]
        probs = jnp.where(allowed, jnp.exp(scores - log_total[:, None]), 0.0)
        dscores = (probs * (dprobs - delta[:, None])).astype(jnp.bfloat16)
        probs_low = probs.astype(jnp.bfloat16)
        grad_query = (
            grad_query
            + jnp.einsum("qk,kd->qd", dscores, key_block, preferred_element_type=jnp.float32)
            * score_scale
        )
        grad_key = (
            jnp.einsum("qk,qd->kd", dscores, queries_all, preferred_element_type=jnp.float32)
            * score_scale
        )
        grad_value = jnp.einsum(
            "qk,qd->kd", probs_low, grads_all, preferred_element_type=jnp.float32
        )
        return (grad_query, (grad_key, grad_value))

    indices = jnp.arange(key_count // block_rows, dtype=jnp.int32)
    inputs = (indices,)
    initial = jnp.zeros(queries_all.shape, jnp.float32)
    grad_query, (grad_key, grad_value) = lax.scan(tile_advance, initial, inputs)
    return (grad_query, grad_key.reshape(key_count, width), grad_value.reshape(key_count, width))


def body(queries, key_rows, value_rows, grad_output, positions):
    score_scale = 1.0 / math.sqrt(queries.shape[1])
    row_index = lax.axis_index("row")
    col_index = lax.axis_index("col")
    row_count = lax.axis_size("row")
    col_count = lax.axis_size("col")
    shard_rows = queries.shape[0]
    position_grid = positions.reshape(row_count, col_count, shard_rows)
    queries_all, grads_all = side_by_side((queries, grad_output), "col", 0, 1)
    keys_all, values_all = side_by_side((key_rows, value_rows), "row", 0, 1)
    query_order = lax.dynamic_index_in_dim(position_grid, row_index, 0, keepdims=False).reshape(-1)
    key_order = lax.dynamic_index_in_dim(position_grid, col_index, 1, keepdims=False).reshape(-1)
    partial_value, saved = local_stats(
        queries_all, grads_all, keys_all, values_all, query_order, key_order, score_scale
    )
    run_max, run_sum, run_dot = combined_all(partial_value, "col", combine_stats)
    log_total = run_max + jnp.log(run_sum)
    delta = run_dot / run_sum
    grad_query, grad_key, grad_value = tile_gradients(
        queries_all,
        grads_all,
        keys_all,
        values_all,
        query_order,
        key_order,
        log_total,
        delta,
        score_scale,
    )
    owned_query = summed_on_arrival(grad_query, "col", 0)
    owned_key, owned_value = in_one_piece((grad_key, grad_value), "row", 0, 1)
    return (
        owned_query.astype(jnp.bfloat16),
        owned_key.astype(jnp.bfloat16),
        owned_value.astype(jnp.bfloat16),
    )


def solution(mesh):
    return jax.shard_map(
        body,
        mesh=mesh,
        in_specs=(
            P(("row", "col"), None),
            P(("row", "col"), None),
            P(("row", "col"), None),
            P(("row", "col"), None),
            P(),
        ),
        out_specs=(P(("row", "col"), None), P(("row", "col"), None), P(("row", "col"), None)),
        check_vma=False,
    )
```

profile of v0, /device:TPU:1, one launch (start us, length us, event | category | flops | bytes accessed | tf_op | source)
XLA Modules:
  0.0 285.0 jit_solution(3250667667070649321)
XLA Ops:
  7.2 1.4 pad_maximum_fusion.2
  8.8 0.8 pad_maximum_fusion.1
  9.6 25.8 %all_gather.6 = bf16[1024,256]{1,0:T(8,128)(2,1)S(1)} all-gather(bf16[128,256]{1,0:T(8,128)(2,1)S(1)} %pad_maximum_fusion.1), channel_id=1, replica_groups=mesh['row'=8,'col'=32] {'row'}, dimensions={0}, use_global_device_ids=true | all-gather | bytes 589824 | tf_op jit(solution)/shard_map/all_gather | solution.py:11
  35.4 34.1 %all-gather.2.cloned.1.call-done = bf16[4096,256]{1,0:T(8,128)(2,1)} async-done(((bf16[128,256]{1,0:T(8,128)(2,1)}), bf16[4096,256]{1,0:T(8,128)(2,1)}) %all-gather.2.cloned.1.call-update) | async-done | bytes 2097168 | tf_op jit(solution)/shard_map/all_gather | solution.py:11
  69.6 1.7 fusion.34
  71.2 15.8 %while.30 = (s32[]{:T(128)}, f32[4096]{0:T(1024)S(1)}, f32[4096]{0:T(1024)S(1)}, f32[4096]{0:T(1024)S(1)}, s32[32,128]{1,0:T(8,128)S(1)}, /*index=5*/s32[2]{0:T(...) while((s32[]{:T(128)}, f32[4096]{0:T(1024)S(1)}, ...), condition=%wide.region_4.5_spmd.clone, body=%wide.region_0.4_spmd.clone.sunk | while | flops 1105227776 | bytes 27879652 | solution.py:119
  72.6 1.4 fusion.69
  74.0 2.9 %fusion.70 = f32[4096]{0:T(1024)S(1)} fusion(bf16[4096,128]{1,0:T(8,128)(2,1)S(1)} %get-tuple-element.482, f32[512,4096]{1,0:T(8,128)S(1)} %get-tuple-element.426, f32[4096]{0:T(1024)S(1)} %select_maximum_fusion.2, s32[4096]{0:T(1024)S(1)} %bitcast.106, s32[512]{0:T(512)S(1)} %dynamic_slice.69, bf16[1024,128]{1,0:T(8,128)(2,1)S(1)} %get-tuple-element.481, ...), kind=kOutput, calls=%fused_computation.4.clone.1 | convolution fusion | flops 549449728 | bytes 9619460 | tf_op jit(solution)/shard_map/while/body/eval_jaxpr/qd,kd->qk/dot_general | solution.py:89
  76.9 2.2 fusion.71
  80.5 1.4 fusion.69
  81.9 2.9 %fusion.70 = f32[4096]{0:T(1024)S(1)} fusion(bf16[4096,128]{1,0:T(8,128)(2,1)S(1)} %get-tuple-element.482, f32[512,4096]{1,0:T(8,128)S(1)} %get-tuple-element.426, f32[4096]{0:T(1024)S(1)} %select_maximum_fusion.2, s32[4096]{0:T(1024)S(1)} %bitcast.106, s32[512]{0:T(512)S(1)} %dynamic_slice.69, bf16[1024,128]{1,0:T(8,128)(2,1)S(1)} %get-tuple-element.481, ...), kind=kOutput, calls=%fused_computation.4.clone.1 | convolution fusion | flops 549449728 | bytes 9619460 | tf_op jit(solution)/shard_map/while/body/eval_jaxpr/qd,kd->qk/dot_general | solution.py:89
  84.8 2.2 fusion.71
  87.7 1.8 broadcast_in_dim.36
  89.5 5.6 %all-to-all-start = ((f32[32,3,4096]{2,1,0:T(4,128)}), f32[32,3,4096]{2,1,0:T(4,128)S(1)}, u32[]{:S(2)}, u32[]{:S(2)}) async-start(f32[32,3,4096]{2,1,0:T(4,128)} %broadcast_in_dim.36), calls=%async_computation | async-start | bytes 4194304 | tf_op jit(solution)/shard_map/all_to_all | solution.py:20
  95.1 51.7 %all-to-all-done = f32[32,3,4096]{2,1,0:T(4,128)S(1)} async-done(((f32[32,3,4096]{2,1,0:T(4,128)}), f32[32,3,4096]{2,1,0:T(4,128)S(1)}, u32[]{:S(2)}, u32[]{:S(2)}) %all-to-all-start) | async-done | bytes 1572896 | tf_op jit(solution)/shard_map/all_to_all | solution.py:20
  146.8 1.9 fusion.33
  149.9 1.3 copy.16
  151.3 0.8 slice.145
  152.9 1.1 multiply_add_fusion
  155.6 1.7 multiply_add_fusion.2
  157.5 1.5 slice.149
  159.0 1.5 slice.148
  160.5 1.6 multiply_add_fusion.4
  162.1 1.4 slice.129
  163.5 1.4 slice.128
  164.9 1.4 slice.151
  166.3 1.4 slice.150
  167.7 0.8 multiply_add_fusion.1
  168.5 1.0 slice.136
  169.5 1.0 slice.135
  170.8 0.9 multiply_add_fusion.5
  172.0 0.9 multiply_add_fusion.6
  172.8 0.8 multiply_add_fusion.7
  173.8 25.9 %while.31 = (s32[]{:T(128)}, f32[4096,128]{1,0:T(8,128)}, f32[2,512,128]{2,1,0:T(8,128)}, f32[2,512,128]{2,1,0:T(8,128)}, s32[32,128]{1,0:T(8,128)S(1)}, /*index...) while((s32[]{:T(128)}, f32[4096,128]{1,0:T(8,128)}, ...), condition=%wide.region_6.7_spmd.clone, body=%wide.region_5.6_spmd.clone.sunk | while | flops 2702770176 | bytes 59693452 | solution.py:168
  175.9 3.3 %bitcast_select_fusion.2 = f32[4096,512]{0,1:T(8,128)S(1)} fusion(bf16[4096,128]{1,0:T(8,128)(2,1)} %get-tuple-element.529, f32[4096]{0:T(1024)S(1)} %get-tuple-element.530, s32[4096]{0:T(1024)S(1)} %bitcast.108, s32[512]{0:T(512)S(1)} %dynamic_slice.74, bf16[1024,128]{1,0:T(8,128)(2,1)S(1)} %get-tuple-element.528, s32[]{:T(128)S(6)} %select_n.55), kind=kOutput, calls=%fused_computation.21.clone.1 | convolution fusion | flops 545259520 | bytes 9603076 | tf_op jit(solution)/shard_map/while/body/eval_jaxpr/qd,kd->qk/dot_general | solution.py:86
  179.2 1.3 fusion.86
  180.5 1.3 fusion.83
  182.0 1.2 fusion.85
  183.3 2.7 fusion.84
  187.9 3.3 %bitcast_select_fusion.2 = f32[4096,512]{0,1:T(8,128)S(1)} fusion(bf16[4096,128]{1,0:T(8,128)(2,1)} %get-tuple-element.529, f32[4096]{0:T(1024)S(1)} %get-tuple-element.530, s32[4096]{0:T(1024)S(1)} %bitcast.108, s32[512]{0:T(512)S(1)} %dynamic_slice.74, bf16[1024,128]{1,0:T(8,128)(2,1)S(1)} %get-tuple-element.528, s32[]{:T(128)S(6)} %select_n.55), kind=kOutput, calls=%fused_computation.21.clone.1 | convolution fusion | flops 545259520 | bytes 9603076 | tf_op jit(solution)/shard_map/while/body/eval_jaxpr/qd,kd->qk/dot_general | solution.py:86
  191.2 1.3 fusion.86
  192.5 1.3 fusion.83
  194.1 1.2 fusion.85
  195.3 4.5 %fusion.84 = f32[4096,128]{1,0:T(8,128)} fusion(bf16[4096,512]{0,1:T(8,128)(2,1)S(1)} %fusion.83, f32[4096,128]{1,0:T(8,128)} %get-tuple-element.505, pred[]{:T(512)S(6)} %compare.7, bf16[1024,128]{1,0:T(8,128)(2,1)S(1)} %get-tuple-element.528, s32[]{:T(128)S(6)} %select_n.55), kind=kOutput, calls=%fused_computation.23.clone.1 | convolution fusion | flops 538443776 | bytes 8519685 | tf_op jit(solution)/shard_map/while/body/eval_jaxpr/qk,kd->qd/dot_general | solution.py:153
  199.8 1.3 pad_maximum_fusion
  201.1 18.2 %all_to_all.15 = f32[8,128,256]{2,1,0:T(8,128)S(1)} all-to-all(f32[8,128,256]{2,1,0:T(8,128)S(1)} %pad_maximum_fusion), channel_id=1, replica_groups=mesh['row'=8,'col'=32] {'row'}, dimensions={0} | all-to-all | bytes 2097152 | tf_op jit(solution)/shard_map/all_to_all | solution.py:62
  219.3 6.4 %all-to-all-start.1 = ((f32[32,128,128]{2,1,0:T(8,128)}), f32[32,128,128]{2,1,0:T(8,128)S(1)}, u32[]{:S(2)}, u32[]{:S(2)}) async-start(f32[32,128,128]{2,1,0:T(8,128)} %bitcast.10), calls=%async_computation.1 | async-start | bytes 4194304 | tf_op jit(solution)/shard_map/all_to_all | solution.py:62
  226.4 51.0 %all-to-all-done.1 = f32[32,128,128]{2,1,0:T(8,128)S(1)} async-done(((f32[32,128,128]{2,1,0:T(8,128)}), f32[32,128,128]{2,1,0:T(8,128)S(1)}, u32[]{:S(2)}, u32[]{:S(2)}) %all-to-all-start.1) | async-done | bytes 2097184 | tf_op jit(solution)/shard_map/all_to_all | solution.py:62
  (80 shorter events, 11.1 us)
Async XLA Ops:
  7.2 1.6 copy-start
  7.2 62.4 %all-gather.2.cloned.1.call-start = ((), (), s32[]{:S(2)}) async-start(), calls=%async_computation.3 | async-start | bytes 2162688 | tf_op jit(solution)/shard_map/all_gather | solution.py:11
  87.1 0.6 copy-start.9
  87.1 2.4 copy-start.1
  87.1 2.4 copy-start.3
  89.5 57.3 %all-to-all-start = ((f32[32,3,4096]{2,1,0:T(4,128)}), f32[32,3,4096]{2,1,0:T(4,128)S(1)}, u32[]{:S(2)}, u32[]{:S(2)}) async-start(f32[32,3,4096]{2,1,0:T(4,128)} %broadcast_in_dim.36), calls=%async_computation | async-start | bytes 4194304 | tf_op jit(solution)/shard_map/all_to_all | solution.py:20
  148.7 25.1 %copy-start.2 = (bf16[1024,128]{1,0:T(8,128)(2,1)S(1)}, bf16[1024,128]{1,0:T(8,128)(2,1)}, u32[]{:S(2)}) copy-start(bf16[1024,128]{1,0:T(8,128)(2,1)} %copy-done.1) | copy-start | bytes 786436
  175.9 3.3 %copy-start.5 = (f32[2,512,128]{2,1,0:T(8,128)S(1)}, f32[2,512,128]{2,1,0:T(8,128)}, u32[]{:S(2)}) copy-start(f32[2,512,128]{2,1,0:T(8,128)} %get-tuple-element.507) | copy-start | bytes 1572868 | tf_op jit(solution)/shard_map/while
  180.4 2.8 copy-start.6
  180.4 1.4 copy-start.4
  180.5 1.5 copy-start.7
  183.3 2.7 copy-start.8
  187.9 3.3 %copy-start.5 = (f32[2,512,128]{2,1,0:T(8,128)S(1)}, f32[2,512,128]{2,1,0:T(8,128)}, u32[]{:S(2)}) copy-start(f32[2,512,128]{2,1,0:T(8,128)} %get-tuple-element.507) | copy-start | bytes 1572868 | tf_op jit(solution)/shard_map/while
  192.5 2.8 copy-start.6
  192.5 1.4 copy-start.4
  192.5 1.5 copy-start.7
  195.3 4.5 %copy-start.8 = (f32[2,512,128]{2,1,0:T(8,128)}, f32[2,512,128]{2,1,0:T(8,128)S(1)}, u32[]{:S(2)}) copy-start(f32[2,512,128]{2,1,0:T(8,128)S(1)} %fusion.85) | copy-start | bytes 1572868 | tf_op jit(solution)/shard_map/while
  219.3 58.2 %all-to-all-start.1 = ((f32[32,128,128]{2,1,0:T(8,128)}), f32[32,128,128]{2,1,0:T(8,128)S(1)}, u32[]{:S(2)}, u32[]{:S(2)}) async-start(f32[32,128,128]{2,1,0:T(8,128)} %bitcast.10), calls=%async_computation.1 | async-start | bytes 4194304 | tf_op jit(solution)/shard_map/all_to_all | solution.py:62
Sparse Core Ops, SparseCore 0:
  10.5 58.9 all-gather.1
where the time goes:
time: 286 us; the launch traced here: 285 us
  waiting for transfers between devices  137 us (48%)
  blocking collectives  44.1 us (15%)
  matrix products  30 us (10%)
  local copies, waits for them, and re-layouts  28.1 us (10%)
  other arithmetic  16.7 us (6%)
  between operations  14.4 us (5%)
  starting transfers between devices  12 us (4%)
  loops' own time  2.92 us (1%)
    all_to_all x1, waiting for transfers between devices, sent_to_all(): lax.all_to_all(jnp.broadcast_to(array[None], (devices, *array.shape)), ax...  51.7 us
    all_to_all x1, waiting for transfers between devices, summed_on_arrival(): lax.all_to_all(cut_along(array, dim, devices), axis, 0, 0, tiled=True)  51 us
    all_gather x1, waiting for transfers between devices, side_by_side(): out, at, outs = (lax.all_gather(both, axis, axis=dim, tiled=True), 0, [])  34.1 us
    all_gather x1, blocking collectives, side_by_side(): out, at, outs = (lax.all_gather(both, axis, axis=dim, tiled=True), 0, [])  25.8 us
    all_to_all x1, blocking collectives, summed_on_arrival(): lax.all_to_all(cut_along(array, dim, devices), axis, 0, 0, tiled=True)  18.2 us
    slice x24, local copies, waits for them, and re-layouts, joined_by_halves(): part[side::2]  15.1 us
    dot_general x4, matrix products, block_products(): jnp.einsum('qd,kd->qk', queries_all, key_block, preferred_element_type=jn...  9.35 us
    dot_general x4, matrix products, block_products(): jnp.einsum('qd,kd->qk', grads_all, value_block, preferred_element_type=jn...  8.45 us
  transfers between devices with their start and end apart: 3, of which 3 were waited for; matrix products, arithmetic and copies ran while one was open for 1% of the time, Pallas kernels for 0%

commit v1 on v0

v1 whole, which is shorter than its diff:
```python
import math

import jax
import jax.numpy as jnp
from jax import lax
from jax.experimental import pallas as pl
from jax.experimental.pallas import tpu as pltpu
from jax.sharding import PartitionSpec as P

MESH = pl.DeviceIdType.MESH
F32 = jnp.float32
BF16 = jnp.bfloat16
B = 128
NEG = -1e30
FLOOR = -1e6
LOG2E = math.log2(math.e)


def device(x, y, z, c):
    return (y * 2 + lax.rem(z, 2), (x * 4 + lax.div(z, 2)) * 2 + c)


def nt(a, b):
    return lax.dot_general(a, b, (((1,), (1,)), ((), ())), preferred_element_type=F32)


def nn(a, b):
    return jnp.dot(a, b, preferred_element_type=F32)


def kernel(
    q_ref, k_ref, v_ref, g_ref, pos_ref, dq_ref, dk_ref, dv_ref,
    qb, gb, kb, vb, ktb, posk, posq, w_buf, dp_buf, mt, stat_out, stat_in, lse, dlt,
    dqt, part, tmp, pair_out, pair_in, z_out, z_in, q_out, q_in,
    gs, gr, ss, sr, ps, pr, zs, zr, qs_sem, qr_sem,
):
    row, col = lax.axis_index("row"), lax.axis_index("col")
    y, zlo = lax.div(row, 2), lax.rem(row, 2)
    x, c = lax.div(col, 8), lax.rem(col, 2)
    z = lax.rem(lax.div(col, 2), 4) * 2 + zlo
    up4 = lambda a, d: lax.rem(a + d, 4)
    up8 = lambda a, d: lax.rem(a + d, 8)
    other = 1 - c
    mine = x * 4 + y
    chip_scale = LOG2E / math.sqrt(B)

    plane = [lax.rem(mine + d, 16) for d in range(1, 16)]
    plane_dev = [device(lax.div(s, 4), lax.rem(s, 4), z, c) for s in plane]
    barrier = pltpu.get_barrier_semaphore()
    peers = list(plane_dev) + [device(x, y, z, other)]
    peers += [device(x, y, up8(z, d), c) for d in range(1, 8)]
    for p in peers:
        pl.semaphore_signal(barrier, inc=1, device_id=p, device_id_type=MESH)
    pl.semaphore_wait(barrier, len(peers))

    sent = []

    def send(src, dst, send_sem, recv_sem, to):
        copy = pltpu.make_async_remote_copy(
            src_ref=src, dst_ref=dst, send_sem=send_sem, recv_sem=recv_sem, device_id=to, device_id_type=MESH
        )
        copy.start()
        sent.append(copy)
        return copy

    count = [0]

    def gsend(src, dst, to):
        i = count[0]
        count[0] += 1
        return send(src, dst, gs.at[i], gr.at[i], to)

    slot = lambda a, b: a * 4 + b
    xr, xl, yr, yl = up4(x, 1), up4(x, 3), up4(y, 1), up4(y, 3)
    x2, y2 = up4(x, 2), up4(y, 2)
    to_xr, to_xl = device(xr, y, z, c), device(xl, y, z, c)
    to_yr, to_yl = device(x, yr, z, c), device(x, yl, z, c)
    to_zr, to_zl = device(x, y, up8(z, 1), c), device(x, y, up8(z, 7), c)
    to_pair = device(x, y, z, other)
    half0, half1 = pl.ds(0, 64), pl.ds(64, 64)

    plans = []
    for buf, own, first in ((qb, q_ref, True), (gb, g_ref, False)):
        if first:
            at = lambda i, j: slot(i, j)
            a, b, ar, al, br, bl, a2, b2 = x, y, xr, xl, yr, yl, x2, y2
            to_ar, to_al, to_br, to_bl = to_xr, to_xl, to_yr, to_yl
        else:
            at = lambda i, j: slot(j, i)
            a, b, ar, al, br, bl, a2, b2 = y, x, yr, yl, xr, xl, y2, x2
            to_ar, to_al, to_br, to_bl = to_yr, to_yl, to_xr, to_xl
        plans.append((buf, own, at, a, b, ar, al, br, bl, a2, b2, to_ar, to_al, to_br, to_bl))

    zin_r, zin_l = {}, {}
    kv = ((kb, k_ref), (vb, v_ref))
    kslot = lambda zz, cc: zz * 2 + cc
    pair_copies = []
    state = []
    for buf, own, at, a, b, ar, al, br, bl, a2, b2, to_ar, to_al, to_br, to_bl in plans:
        here = buf.at[at(a, b)]
        state.append(
            dict(
                r=gsend(own, here, to_ar),
                l=gsend(own, here, to_al),
                ups=[gsend(own, here, to_br)],
                downs=[gsend(own, here, to_bl)],
            )
        )
    for w, (buf, own) in enumerate(kv):
        here = buf.at[kslot(z, c)]
        zin_r[w, 1] = gsend(own, here, to_zr)
        zin_l[w, 1] = gsend(own, here, to_zl)
        pair_copies.append(gsend(own, here, to_pair))

    qb[mine] = q_ref[...]
    gb[mine] = g_ref[...]
    kb[kslot(z, c)] = k_ref[...]
    vb[kslot(z, c)] = v_ref[...]
    zhi_col = lax.div(z, 2) * 2 + c
    for s in range(16):
        i, j = s // 4, s % 4
        posq[pl.ds(s, 1), :] = pos_ref[pl.ds((j * 2 + zlo) * 32 + i * 8 + zhi_col, 1), :].astype(F32)
    for s in range(16):
        zz, cc = s // 2, s % 2
        line = pos_ref[pl.ds((y * 2 + zz % 2) * 32 + (x * 4 + zz // 2) * 2 + cc, 1), :].astype(F32)
        posk[s] = jnp.broadcast_to(line, (B, B)).T

    def forward_kv(h):
        for w, (buf, _) in enumerate(kv):
            from_l = zin_r.get((w, h))
            from_r = zin_l.get((w, h))
            if from_l is not None:
                from_l.wait_recv()
                src = buf.at[kslot(up8(z, 8 - h), c)]
                if h < 3 or (h == 3 and w == 0):
                    zin_r[w, h + 1] = gsend(src, src, to_zr)
                pair_copies.append(gsend(src, src, to_pair))
            if from_r is not None:
                from_r.wait_recv()
                src = buf.at[kslot(up8(z, h), c)]
                if h < 3 or (h == 3 and w == 1):
                    zin_l[w, h + 1] = gsend(src, src, to_zl)
                pair_copies.append(gsend(src, src, to_pair))

    for st, (buf, own, at, a, b, ar, al, br, bl, a2, b2, to_ar, to_al, to_br, to_bl) in zip(state, plans):
        st["r"].wait_recv()
        src = buf.at[at(al, b)]
        st["r2"] = gsend(src.at[half0], src.at[half0], to_ar)
        st["ups"].append(gsend(src, src, to_br))
        st["downs"].append(gsend(src, src, to_bl))
        st["l"].wait_recv()
        src = buf.at[at(ar, b)]
        st["l2"] = gsend(src.at[half1], src.at[half1], to_al)
        st["ups"].append(gsend(src, src, to_br))
        st["downs"].append(gsend(src, src, to_bl))
    forward_kv(1)
    for st, (buf, own, at, a, b, ar, al, br, bl, a2, b2, to_ar, to_al, to_br, to_bl) in zip(state, plans):
        st["r2"].wait_recv()
        st["l2"].wait_recv()
        src = buf.at[at(a2, b)]
        st["ups"].append(gsend(src, src, to_br))
        st["downs"].append(gsend(src, src, to_bl))
    forward_kv(2)
    last = []
    for st, (buf, own, at, a, b, ar, al, br, bl, a2, b2, to_ar, to_al, to_br, to_bl) in zip(state, plans):
        for n, ia in enumerate((a, al, ar, a2)):
            st["ups"][n].wait_recv()
            src = buf.at[at(ia, bl)]
            last.append(gsend(src.at[half0], src.at[half0], to_br))
            st["downs"][n].wait_recv()
            src = buf.at[at(ia, br)]
            last.append(gsend(src.at[half1], src.at[half1], to_bl))
    forward_kv(3)
    forward_kv(4)
    for copy in last:
        copy.wait_recv()
    for copy in pair_copies:
        copy.wait_recv()

    for zz in range(8):
        ktb[zz] = kb[pl.ds(2 * zz, 2)].reshape(2 * B, B).T

    def scores(t, carry):
        q_tile = qb[pl.ds(4 * t, 4)].reshape(4 * B, B)
        g_tile = gb[pl.ds(4 * t, 4)].reshape(4 * B, B)
        pq = jnp.concatenate([posq[pl.ds(4 * t + j, 1), :] for j in range(4)], axis=1)
        maxes, sums, dots = [], [], []
        for zz in range(8):
            k_tile = kb[2 * zz : 2 * zz + 2].reshape(2 * B, B)
            v_tile = vb[2 * zz : 2 * zz + 2].reshape(2 * B, B)
            s = nt(k_tile, q_tile)
            dp = nt(v_tile, g_tile)
            pk = posk[2 * zz : 2 * zz + 2].reshape(2 * B, B)
            pk = jnp.concatenate([pk] * 4, axis=1)
            s = jnp.where(pq >= pk, s, NEG)
            m = jnp.maximum(jnp.max(s, axis=0, keepdims=True), FLOOR)
            w = jnp.exp2((s - m) * chip_scale)
            w_buf[t, zz] = w
            dp_buf[t, zz] = dp
            mt[t, pl.ds(zz, 1), :] = m * chip_scale
            maxes.append(m)
            sums.append(jnp.sum(w, axis=0, keepdims=True))
            dots.append(jnp.sum(w * dp, axis=0, keepdims=True))
        top = maxes[0]
        for m in maxes[1:]:
            top = jnp.maximum(top, m)
        total = jnp.zeros_like(top)
        dot = jnp.zeros_like(top)
        for m, a, d in zip(maxes, sums, dots):
            f = jnp.exp2((m - top) * chip_scale)
            total += a * f
            dot += d * f
        some = total > 0.0
        safe = jnp.where(some, total, 1.0)
        level = jnp.where(some, top * chip_scale + jnp.log(safe) * LOG2E, NEG)
        mean = dot / safe
        for j in range(4):
            stat_out[t, pl.ds(j, 1), :] = level[:, j * B : (j + 1) * B]
            stat_out[t, pl.ds(4 + j, 1), :] = mean[:, j * B : (j + 1) * B]
        stat_in[t, mine] = stat_out[t]
        for d in range(15):
            pltpu.make_async_remote_copy(
                src_ref=stat_out.at[t], dst_ref=stat_in.at[t, mine], send_sem=ss.at[t, d], recv_sem=sr.at[t, d],
                device_id=plane_dev[d], device_id_type=MESH,
            ).start()
        return carry

    lax.fori_loop(0, 4, scores, 0)

    def combine(t, carry):
        for d in range(15):
            copy = pltpu.make_async_remote_copy(
                src_ref=stat_out.at[t], dst_ref=stat_in.at[t, lax.rem(mine + 15 - d, 16)], send_sem=ss.at[t, d],
                recv_sem=sr.at[t, d], device_id=plane_dev[d], device_id_type=MESH,
            )
            copy.wait_recv()
            copy.wait_send()
        level = stat_in[t, :, 0:4, :]
        mean = stat_in[t, :, 4:8, :]
        top = jnp.max(level, axis=0)
        e = jnp.exp2(level - top[None])
        total = jnp.sum(e, axis=0)
        lse[t] = top + jnp.log(total) * LOG2E
        dlt[t] = jnp.sum(e * mean, axis=0) / total
        return carry

    lax.fori_loop(0, 4, combine, 0)

    def pair_copy(zz):
        return pltpu.make_async_remote_copy(
            src_ref=pair_out.at[zz], dst_ref=pair_in.at[zz], send_sem=ps.at[zz], recv_sem=pr.at[zz],
            device_id=to_pair, device_id_type=MESH,
        )

    def z_copy(zz):
        return pltpu.make_async_remote_copy(
            src_ref=z_out.at[zz], dst_ref=z_in.at[z], send_sem=zs.at[zz], recv_sem=zr.at[z],
            device_id=device(x, y, zz, c), device_id_type=MESH,
        )

    def order(i):
        h = lax.div(i + 1, 2)
        return up8(z, 4 + jnp.where(lax.rem(i, 2) == 1, -h, h))

    def pass_on(zz):
        pair_copy(zz).wait_recv()
        z_out[zz] = (part[zz] + pair_in[zz].astype(F32)).astype(BF16)
        z_copy(zz).start()

    dqt[...] = jnp.zeros_like(dqt)

    def gradients(i, carry):
        zz = order(i)
        k_cols = ktb[zz]
        dk = jnp.zeros((2 * B, B), F32)
        dv = jnp.zeros((2 * B, B), F32)
        for t in range(4):
            level = jnp.concatenate([lse[t, j : j + 1, :] for j in range(4)], axis=1)
            mean = jnp.concatenate([dlt[t, j : j + 1, :] for j in range(4)], axis=1)
            f = jnp.exp2(mt[t, pl.ds(zz, 1), :] - level)
            p = w_buf[t, zz] * f
            ds = (p * (dp_buf[t, zz] - mean)).astype(BF16)
            dv += nn(p.astype(BF16), gb[4 * t : 4 * t + 4].reshape(4 * B, B))
            dk += nn(ds, qb[4 * t : 4 * t + 4].reshape(4 * B, B))
            dqt[t] += nn(k_cols, ds)
        tmp[0] = dk.reshape(2, B, B)
        tmp[1] = dv.reshape(2, B, B)
        part[zz, 0] = tmp[0, c]
        part[zz, 1] = tmp[1, c]
        pair_out[zz, 0] = tmp[0, other].astype(BF16)
        pair_out[zz, 1] = tmp[1, other].astype(BF16)
        pair_copy(zz).start()

        @pl.when(i > 0)
        def _():
            pass_on(order(i - 1))

        return carry

    lax.fori_loop(0, 8, gradients, 0)

    def q_copy(d):
        s = plane[d]
        return pltpu.make_async_remote_copy(
            src_ref=q_out.at[s], dst_ref=q_in.at[mine], send_sem=qs_sem.at[d], recv_sem=qr_sem.at[d],
            device_id=plane_dev[d], device_id_type=MESH,
        )

    for s in range(16):
        q_out[s] = dqt[s // 4, :, (s % 4) * B : (s % 4 + 1) * B].astype(BF16)
    for d in range(15):
        q_copy(d).start()

    scale = 1.0 / math.sqrt(B)
    pair_copy(z).wait_recv()
    acc = part[z] + pair_in[z].astype(F32)
    for d in range(1, 8):
        src = up8(z, 8 - d)
        pltpu.make_async_remote_copy(
            src_ref=z_out.at[src], dst_ref=z_in.at[src], send_sem=zs.at[src], recv_sem=zr.at[src],
            device_id=device(x, y, src, c), device_id_type=MESH,
        ).wait_recv()
        acc += z_in[src].astype(F32)
    dk_ref[...] = (acc[0] * scale).astype(BF16)
    dv_ref[...] = acc[1].astype(BF16)

    own = q_out[mine].astype(F32)
    for d in range(15):
        q_copy(d).wait_recv()
        own += q_in[lax.rem(mine + 15 - d, 16)].astype(F32)
    dq_ref[...] = (own * scale).T.astype(BF16)

    for copy in sent:
        copy.wait_send()
    for zz in range(8):
        pair_copy(zz).wait_send()
    for d in range(1, 8):
        z_copy(up8(z, d)).wait_send()
    for d in range(15):
        q_copy(d).wait_send()


def body(queries, key_rows, value_rows, grad_output, positions):
    vmem = pl.BlockSpec(memory_space=pltpu.VMEM)
    out = jax.ShapeDtypeStruct((B, B), BF16)
    dma = pltpu.SemaphoreType.DMA
    blocks = pltpu.VMEM((16, B, B), BF16)
    return pl.pallas_call(
        kernel,
        out_shape=(out, out, out),
        in_specs=[vmem] * 5,
        out_specs=(vmem,) * 3,
        scratch_shapes=[
            blocks, blocks, blocks, blocks,
            pltpu.VMEM((8, B, 2 * B), BF16),
            pltpu.VMEM((16, B, B), F32),
            pltpu.VMEM((16, B), F32),
            pltpu.VMEM((4, 8, 2 * B, 4 * B), F32),
            pltpu.VMEM((4, 8, 2 * B, 4 * B), F32),
            pltpu.VMEM((4, 8, 4 * B), F32),
            pltpu.VMEM((4, 8, B), F32),
            pltpu.VMEM((4, 16, 8, B), F32),
            pltpu.VMEM((4, 4, B), F32),
            pltpu.VMEM((4, 4, B), F32),
            pltpu.VMEM((4, B, 4 * B), F32),
            pltpu.VMEM((8, 2, B, B), F32),
            pltpu.VMEM((2, 2, B, B), F32),
            pltpu.VMEM((8, 2, B, B), BF16),
            pltpu.VMEM((8, 2, B, B), BF16),
            pltpu.VMEM((8, 2, B, B), BF16),
            pltpu.VMEM((8, 2, B, B), BF16),
            pltpu.VMEM((16, B, B), BF16),
            pltpu.VMEM((16, B, B), BF16),
            dma((70,)), dma((70,)),
            dma((4, 15)), dma((4, 15)),
            dma((8,)), dma((8,)),
            dma((8,)), dma((8,)),
            dma((15,)), dma((15,)),
        ],
        compiler_params=pltpu.CompilerParams(
            collective_id=0, has_side_effects=True, vmem_limit_bytes=60 * 1024 * 1024
        ),
        name="attention_backward",
    )(queries, key_rows, value_rows, grad_output, positions.reshape(-1, B))


def solution(mesh):
    spec = P(("row", "col"), None)
    return jax.shard_map(
        body,
        mesh=mesh,
        in_specs=(spec, spec, spec, spec, P()),
        out_specs=(spec, spec, spec),
        check_vma=False,
    )
```

time: 286 us -> 64.6 us (0.23)
  waiting for transfers between devices: 137 us -> 0 us
  Pallas kernels: 0 us -> 60.9 us
  blocking collectives: 44.1 us -> 0 us
  matrix products: 30 us -> 0 us
  local copies, waits for them, and re-layouts: 28.1 us -> 2.77 us
  other arithmetic: 16.7 us -> 0 us
  between operations: 14.4 us -> 0.65 us
  starting transfers between devices: 12 us -> 0 us
  loops' own time: 2.92 us -> 0 us
    all_to_all x2 -> x0, waiting for transfers between devices: 103 us -> none  [the longest x1 51.7 us: sent_to_all(): lax.all_to_all(jnp.broadcast_to(array[None], (devices, *array.shape)), ax...]
    pallas_call x0 -> x1, Pallas kernels: none -> 60.9 us  [body(): pl.pallas_call(kernel, out_shape=(out, out, out), in_specs=[vmem] * 5, ou...]
    all_gather x1 -> x0, waiting for transfers between devices: 34.1 us -> none  [side_by_side(): out, at, outs = (lax.all_gather(both, axis, axis=dim, tiled=True), 0, [])]
    dot_general x14 -> x0, matrix products: 30 us -> none  [the longest x4 9.35 us: block_products(): jnp.einsum('qd,kd->qk', queries_all, key_block, preferred_element_type=jn...]
    all_gather x1 -> x0, blocking collectives: 25.8 us -> none  [side_by_side(): out, at, outs = (lax.all_gather(both, axis, axis=dim, tiled=True), 0, [])]
    slice x27 -> x0, local copies, waits for them, and re-layouts: 18.7 us -> none  [the longest x24 15.1 us: joined_by_halves(): part[side::2]]
    all_to_all x1 -> x0, blocking collectives: 18.2 us -> none  [summed_on_arrival(): lax.all_to_all(cut_along(array, dim, devices), axis, 0, 0, tiled=True)]
    all_to_all x2 -> x0, starting transfers between devices: 12 us -> none  [the longest x1 6.41 us: summed_on_arrival(): lax.all_to_all(cut_along(array, dim, devices), axis, 0, 0, tiled=True)]
  transfers between devices with their start and end apart: 3 -> 0, of which waited for: 3 -> 0; matrix products, arithmetic and copies ran while one was open for 1% -> 0% of each run, Pallas kernels for 0% -> 0%
where the time goes in v1:
time: 64.6 us; the launch traced here: 64.4 us
  Pallas kernels  60.9 us (94%)
  local copies, waits for them, and re-layouts  2.77 us (4%)
  between operations  0.65 us (1%)
    pallas_call x1, Pallas kernels, body(): pl.pallas_call(kernel, out_shape=(out, out, out), in_specs=[vmem] * 5, ou...  60.9 us
    unnamed x7, local copies, waits for them, and re-layouts  2.77 us

profile of v1, /device:TPU:1, one launch (start us, length us, event | category | flops | bytes accessed | tf_op | source)
XLA Modules:
  0.0 64.4 jit_solution(2222122596835620644)
XLA Ops:
  0.6 60.9 %attention_backward.1 = (bf16[128,128]{1,0:T(8,128)(2,1)}, bf16[128,128]{1,0:T(8,128)(2,1)}, bf16[128,128]{1,0:T(8,128)(2,1)}) custom-call(bf16[128,128]{1,0:T(8,128)(2,1)} %q_ref.1, bf16[128,128]{1,0:T(8,128)(2,1)} %k_ref.1, bf16[128,128]{1,0:T(8,128)(2,1)} %v_ref.1, bf16[128,128]{1,0:T(8,128)(2,1)} %g_ref.1, s32[256,128]{1,0:T(8,128)} %bitcast.1), custom_call_target="tpu_custom_call" | custom-call | tf_op jit(solution)/shard_map/attention_backward/pallas_call | solution.py:348
  61.6 0.0 copy-start.1
  61.6 1.4 %copy.11 = bf16[128,128]{1,0:T(8,128)(2,1)} copy(bf16[128,128]{1,0:T(8,128)(2,1)} %get-tuple-element.6) | data formatting | bytes 65536
  63.0 0.0 copy-done.1
  63.0 0.0 copy-start
  63.0 0.6 copy.12
  63.6 0.2 copy-done
  63.7 0.6 copy.13
Async XLA Ops:
  61.6 1.4 %copy-start.1 = (bf16[128,128]{1,0:T(8,128)(2,1)S(1)}, bf16[128,128]{1,0:T(8,128)(2,1)}, u32[]{:S(2)}) copy-start(bf16[128,128]{1,0:T(8,128)(2,1)} %get-tuple-element.7) | copy-start | bytes 98308
  63.0 0.8 %copy-start = (bf16[128,128]{1,0:T(8,128)(2,1)S(1)}, bf16[128,128]{1,0:T(8,128)(2,1)}, u32[]{:S(2)}) copy-start(bf16[128,128]{1,0:T(8,128)(2,1)} %get-tuple-element.8) | copy-start | bytes 98308

commit v2 on v1

v2 whole, which is shorter than its diff:
```python
import math

import jax
import jax.numpy as jnp
from jax import lax
from jax.experimental import pallas as pl
from jax.experimental.pallas import tpu as pltpu
from jax.sharding import PartitionSpec as P

MESH = pl.DeviceIdType.MESH
F32 = jnp.float32
BF16 = jnp.bfloat16
B = 128
NEG = -1e30
FLOOR = -1e6
LOG2E = math.log2(math.e)


def device(x, y, z, c):
    return (y * 2 + lax.rem(z, 2), (x * 4 + lax.div(z, 2)) * 2 + c)


def nt(a, b):
    return lax.dot_general(a, b, (((1,), (1,)), ((), ())), preferred_element_type=F32)


def nn(a, b):
    return jnp.dot(a, b, preferred_element_type=F32)


def kernel(
    q_ref, k_ref, v_ref, g_ref, pos_hbm, out_ref,
    qb, gb, kb, vb, pos_ref, ktb, posk, posq, s_buf, dp_buf, mt, zt, dt, stat_out, stat_in, lse, dlt,
    dqt, part, tmp, pair_out, pair_in, z_out, z_in, q_out, q_in,
    ins, gs, gr, ss, sr, ps, pr, zs, zr, qs_sem, qr_sem,
):
    row, col = lax.axis_index("row"), lax.axis_index("col")
    y, zlo = lax.div(row, 2), lax.rem(row, 2)
    x, c = lax.div(col, 8), lax.rem(col, 2)
    z = lax.rem(lax.div(col, 2), 4) * 2 + zlo
    up4 = lambda a, d: lax.rem(a + d, 4)
    up8 = lambda a, d: lax.rem(a + d, 8)
    other = 1 - c
    mine = x * 4 + y
    chip_scale = LOG2E / math.sqrt(B)

    here_k = z * 2 + c
    fetch = [
        pltpu.make_async_copy(src, dst, ins.at[n])
        for n, (src, dst) in enumerate(
            ((k_ref, kb.at[here_k]), (v_ref, vb.at[here_k]), (q_ref, qb.at[mine]), (g_ref, gb.at[mine]), (pos_hbm, pos_ref))
        )
    ]
    for copy in fetch:
        copy.start()

    plane = [lax.rem(mine + d, 16) for d in range(1, 16)]
    plane_dev = [device(lax.div(s, 4), lax.rem(s, 4), z, c) for s in plane]
    barrier = pltpu.get_barrier_semaphore()
    peers = [device(up4(x, d), y, z, c) for d in (1, 3)] + [device(x, up4(y, d), z, c) for d in (1, 3)]
    peers += [device(x, y, up8(z, d), c) for d in (1, 7)] + [device(x, y, z, other)]
    for p in peers:
        pl.semaphore_signal(barrier, inc=1, device_id=p, device_id_type=MESH)
    for copy in fetch[:4]:
        copy.wait()
    pl.semaphore_wait(barrier, len(peers))

    sent = []

    def send(src, dst, send_sem, recv_sem, to):
        copy = pltpu.make_async_remote_copy(
            src_ref=src, dst_ref=dst, send_sem=send_sem, recv_sem=recv_sem, device_id=to, device_id_type=MESH
        )
        copy.start()
        sent.append(copy)
        return copy

    count = [0]

    def gsend(src, dst, to):
        i = count[0]
        count[0] += 1
        return send(src, dst, gs.at[i], gr.at[i], to)

    slot = lambda a, b: a * 4 + b
    xr, xl, yr, yl = up4(x, 1), up4(x, 3), up4(y, 1), up4(y, 3)
    x2, y2 = up4(x, 2), up4(y, 2)
    to_xr, to_xl = device(xr, y, z, c), device(xl, y, z, c)
    to_yr, to_yl = device(x, yr, z, c), device(x, yl, z, c)
    to_zr, to_zl = device(x, y, up8(z, 1), c), device(x, y, up8(z, 7), c)
    to_pair = device(x, y, z, other)
    half0, half1 = pl.ds(0, 64), pl.ds(64, 64)

    done = set()

    def need(*copies):
        for copy in copies:
            if id(copy) not in done:
                done.add(id(copy))
                copy.wait_recv()

    plans = []
    for buf, first in ((qb, True), (gb, False)):
        if first:
            at = lambda i, j: slot(i, j)
            a, b, ar, al, br, bl, a2 = x, y, xr, xl, yr, yl, x2
            to_ar, to_al, to_br, to_bl = to_xr, to_xl, to_yr, to_yl
        else:
            at = lambda i, j: slot(j, i)
            a, b, ar, al, br, bl, a2 = y, x, yr, yl, xr, xl, y2
            to_ar, to_al, to_br, to_bl = to_yr, to_yl, to_xr, to_xl
        plans.append((dict(), buf, at, a, b, ar, al, br, bl, a2, to_ar, to_al, to_br, to_bl))

    zin_r, zin_l, pair = {}, {}, {}
    kv = (kb, vb)
    kslot = lambda zz, cc: zz * 2 + cc

    def forward_kv(h):
        for w, buf in enumerate(kv):
            for came, far, to_next, off in ((zin_r, 0, to_zr, 8 - h), (zin_l, 1, to_zl, h)):
                if h and (w, h) not in came:
                    continue
                if h:
                    need(came[w, h])
                src = buf.at[kslot(up8(z, off % 8), c)]
                if h < 3 or (h == 3 and w == far):
                    came[w, h + 1] = gsend(src, src, to_next)
                if h or not far:
                    pair[w, off % 8] = gsend(src, src, to_pair)

    def across(st, buf, at, ia, b, to_br, to_bl, n):
        src = buf.at[at(ia, b)]
        st["up", n] = gsend(src, src, to_br)
        st["down", n] = gsend(src, src, to_bl)

    def across_last(st, buf, at, ia, br, bl, to_br, to_bl, n):
        need(st["up", n])
        src = buf.at[at(ia, bl)].at[half0]
        st["lu", n] = gsend(src, src, to_br)
        need(st["down", n])
        src = buf.at[at(ia, br)].at[half1]
        st["ld", n] = gsend(src, src, to_bl)

    forward_kv(0)
    for st, buf, at, a, b, ar, al, br, bl, a2, to_ar, to_al, to_br, to_bl in plans:
        src = buf.at[at(a, b)]
        st["r"] = gsend(src, src, to_ar)
        st["l"] = gsend(src, src, to_al)
        across(st, buf, at, a, b, to_br, to_bl, 0)

    fetch[4].wait()
    zhi_col = lax.div(z, 2) * 2 + c
    for s in range(16):
        i, j = s // 4, s % 4
        posq[pl.ds(s, 1), :] = pos_ref[pl.ds((j * 2 + zlo) * 32 + i * 8 + zhi_col, 1), :].astype(F32)
    for s in range(16):
        zz, cc = s // 2, s % 2
        line = pos_ref[pl.ds((y * 2 + zz % 2) * 32 + (x * 4 + zz // 2) * 2 + cc, 1), :].astype(F32)
        posk[s] = jnp.broadcast_to(line, (B, B)).T

    def tile(t, zz):
        q_tile = qb[pl.ds(4 * t, 4)].reshape(4 * B, B)
        g_tile = gb[pl.ds(4 * t, 4)].reshape(4 * B, B)
        k_tile = kb[pl.ds(2 * zz, 2)].reshape(2 * B, B)
        v_tile = vb[pl.ds(2 * zz, 2)].reshape(2 * B, B)
        pq = jnp.concatenate([posq[pl.ds(4 * t + j, 1), :] for j in range(4)], axis=1)
        pk = posk[pl.ds(2 * zz, 2)].reshape(2 * B, B)
        pk = jnp.concatenate([pk] * 4, axis=1)
        s = jnp.where(pq >= pk, nt(k_tile, q_tile), NEG)
        s_buf[t, zz] = s
        m = jnp.maximum(jnp.max(s, axis=0, keepdims=True), FLOOR)
        dp = nt(v_tile, g_tile)
        dp_buf[t, zz] = dp
        w = jnp.exp2((s - m) * chip_scale)
        mt[t, pl.ds(zz, 1), :] = m
        zt[t, pl.ds(zz, 1), :] = jnp.sum(w, axis=0, keepdims=True)
        dt[t, pl.ds(zz, 1), :] = jnp.sum(w * dp, axis=0, keepdims=True)

    def tiles(n, pick):
        def step(i, carry):
            for t, zz in pick(i):
                tile(t, zz)
            return carry

        lax.fori_loop(0, n, step, 0)

    near = lambda i: up8(z, i + 5 * lax.div(i, 2))
    both = lambda i, d: up8(z, d + i * (8 - 2 * d))

    forward_kv(1)
    for st, buf, at, a, b, ar, al, br, bl, a2, to_ar, to_al, to_br, to_bl in plans:
        need(st["r"])
        src = buf.at[at(al, b)].at[half0]
        st["r2"] = gsend(src, src, to_ar)
        across(st, buf, at, al, b, to_br, to_bl, 1)
        need(st["l"])
        src = buf.at[at(ar, b)].at[half1]
        st["l2"] = gsend(src, src, to_al)
        across(st, buf, at, ar, b, to_br, to_bl, 2)
        across_last(st, buf, at, a, br, bl, to_br, to_bl, 0)
    forward_kv(2)
    for st, buf, at, a, b, ar, al, br, bl, a2, to_ar, to_al, to_br, to_bl in plans:
        need(st["r2"], st["l2"])
        across(st, buf, at, a2, b, to_br, to_bl, 3)
        across_last(st, buf, at, al, br, bl, to_br, to_bl, 1)
        across_last(st, buf, at, ar, br, bl, to_br, to_bl, 2)
    sq, sg = plans[0][0], plans[1][0]
    need(sq["lu", 0], sq["ld", 0], *(pair[w, off] for w in range(2) for off in (0, 1, 7)))
    tiles(3, lambda i: [(x, near(i))])
    for st, buf, at, a, b, ar, al, br, bl, a2, to_ar, to_al, to_br, to_bl in plans:
        across_last(st, buf, at, a2, br, bl, to_br, to_bl, 3)
    need(*(sq[k, n] for k in ("lu", "ld") for n in (1, 2)))
    tiles(3, lambda i: [(xr, near(i)), (xl, near(i))])
    forward_kv(3)
    need(*(pair[w, off] for w in range(2) for off in (2, 6)))
    tiles(2, lambda i: [(x, both(i, 2)), (xr, both(i, 2)), (xl, both(i, 2))])
    need(*(sq[k, 3] for k in ("lu", "ld")), *(sg[k, n] for k in ("lu", "ld") for n in range(4)))
    tiles(3, lambda i: [(x2, near(i))])
    forward_kv(4)
    tiles(2, lambda i: [(x2, both(i, 2))])
    need(*(pair[w, off] for w in range(2) for off in (3, 5)))
    tiles(4, lambda i: [(i, both(0, 3)), (i, both(1, 3))])
    need(*(pair[w, 4] for w in range(2)))

    def finish(t, carry):
        tile(t, up8(z, 4))
        maxes = mt[t]
        top = jnp.max(maxes, axis=0, keepdims=True)
        f = jnp.exp2((maxes - top) * chip_scale)
        total = jnp.sum(zt[t] * f, axis=0, keepdims=True)
        dot = jnp.sum(dt[t] * f, axis=0, keepdims=True)
        some = total > 0.0
        safe = jnp.where(some, total, 1.0)
        level = jnp.where(some, top * chip_scale + jnp.log(safe) * LOG2E, NEG)
        mean = dot / safe
        for j in range(4):
            stat_out[t, pl.ds(j, 1), :] = level[:, j * B : (j + 1) * B]
            stat_out[t, pl.ds(4 + j, 1), :] = mean[:, j * B : (j + 1) * B]
        stat_in[t, mine] = stat_out[t]
        for d in range(15):
            pltpu.make_async_remote_copy(
                src_ref=stat_out.at[t], dst_ref=stat_in.at[t, mine], send_sem=ss.at[t, d], recv_sem=sr.at[t, d],
                device_id=plane_dev[d], device_id_type=MESH,
            ).start()
        return carry

    lax.fori_loop(0, 4, finish, 0)

    for zz in range(8):
        ktb[zz] = kb[pl.ds(2 * zz, 2)].reshape(2 * B, B).T
    dqt[...] = jnp.zeros_like(dqt)

    def combine(t, carry):
        for d in range(15):
            copy = pltpu.make_async_remote_copy(
                src_ref=stat_out.at[t], dst_ref=stat_in.at[t, lax.rem(mine + 15 - d, 16)], send_sem=ss.at[t, d],
                recv_sem=sr.at[t, d], device_id=plane_dev[d], device_id_type=MESH,
            )
            copy.wait_recv()
            copy.wait_send()
        level = stat_in[t, :, 0:4, :]
        mean = stat_in[t, :, 4:8, :]
        top = jnp.max(level, axis=0)
        e = jnp.exp2(level - top[None])
        total = jnp.sum(e, axis=0)
        lse[t] = top + jnp.log(total) * LOG2E
        dlt[t] = jnp.sum(e * mean, axis=0) / total
        return carry

    lax.fori_loop(0, 4, combine, 0)

    def pair_copy(zz):
        return pltpu.make_async_remote_copy(
            src_ref=pair_out.at[zz], dst_ref=pair_in.at[zz], send_sem=ps.at[zz], recv_sem=pr.at[zz],
            device_id=to_pair, device_id_type=MESH,
        )

    def z_copy(zz):
        return pltpu.make_async_remote_copy(
            src_ref=z_out.at[zz], dst_ref=z_in.at[z], send_sem=zs.at[zz], recv_sem=zr.at[z],
            device_id=device(x, y, zz, c), device_id_type=MESH,
        )

    def order(i):
        h = lax.div(i + 1, 2)
        return up8(z, 4 + jnp.where(lax.rem(i, 2) == 1, -h, h))

    def pass_on(zz):
        pair_copy(zz).wait_recv()
        z_out[zz] = (part[zz] + pair_in[zz].astype(F32)).astype(BF16)
        z_copy(zz).start()

    def gradients(i, carry):
        zz = order(i)
        k_cols = ktb[zz]
        dk = jnp.zeros((2 * B, B), F32)
        dv = jnp.zeros((2 * B, B), F32)
        for t in range(4):
            level = jnp.concatenate([lse[t, j : j + 1, :] for j in range(4)], axis=1)
            mean = jnp.concatenate([dlt[t, j : j + 1, :] for j in range(4)], axis=1)
            p = jnp.exp2(s_buf[t, zz] * chip_scale - level)
            ds = (p * (dp_buf[t, zz] - mean)).astype(BF16)
            dv += nn(p.astype(BF16), gb[4 * t : 4 * t + 4].reshape(4 * B, B))
            dk += nn(ds, qb[4 * t : 4 * t + 4].reshape(4 * B, B))
            dqt[t] += nn(k_cols, ds)
        tmp[0] = dk.reshape(2, B, B)
        tmp[1] = dv.reshape(2, B, B)
        part[zz, 0] = tmp[0, c]
        part[zz, 1] = tmp[1, c]
        pair_out[zz, 0] = tmp[0, other].astype(BF16)
        pair_out[zz, 1] = tmp[1, other].astype(BF16)
        pair_copy(zz).start()

        @pl.when(i > 0)
        def _():
            pass_on(order(i - 1))

        return carry

    lax.fori_loop(0, 8, gradients, 0)

    def q_copy(d):
        s = plane[d]
        return pltpu.make_async_remote_copy(
            src_ref=q_out.at[s], dst_ref=q_in.at[mine], send_sem=qs_sem.at[d], recv_sem=qr_sem.at[d],
            device_id=plane_dev[d], device_id_type=MESH,
        )

    for s in range(16):
        q_out[s] = dqt[s // 4, :, (s % 4) * B : (s % 4 + 1) * B].astype(BF16)
    for d in range(15):
        q_copy(d).start()

    scale = 1.0 / math.sqrt(B)
    pair_copy(z).wait_recv()
    acc = part[z] + pair_in[z].astype(F32)
    for d in range(1, 8):
        src = up8(z, 8 - d)
        pltpu.make_async_remote_copy(
            src_ref=z_out.at[src], dst_ref=z_in.at[src], send_sem=zs.at[src], recv_sem=zr.at[src],
            device_id=device(x, y, src, c), device_id_type=MESH,
        ).wait_recv()
        acc += z_in[src].astype(F32)
    out_ref[1] = (acc[0] * scale).astype(BF16)
    out_ref[2] = acc[1].astype(BF16)

    own = q_out[mine].astype(F32)
    for d in range(15):
        q_copy(d).wait_recv()
        own += q_in[lax.rem(mine + 15 - d, 16)].astype(F32)
    out_ref[0] = (own * scale).T.astype(BF16)

    for copy in sent:
        copy.wait_send()
    for zz in range(8):
        pair_copy(zz).wait_send()
    for d in range(1, 8):
        z_copy(up8(z, d)).wait_send()
    for d in range(15):
        q_copy(d).wait_send()


def body(queries, key_rows, value_rows, grad_output, positions):
    vmem = pl.BlockSpec(memory_space=pltpu.VMEM)
    hbm = pl.BlockSpec(memory_space=pl.ANY)
    dma = pltpu.SemaphoreType.DMA
    blocks = pltpu.VMEM((16, B, B), BF16)
    grads = pl.pallas_call(
        kernel,
        out_shape=jax.ShapeDtypeStruct((3, B, B), BF16),
        in_specs=[hbm] * 5,
        out_specs=vmem,
        scratch_shapes=[
            blocks, blocks, blocks, blocks,
            pltpu.VMEM((256, B), jnp.int32),
            pltpu.VMEM((8, B, 2 * B), BF16),
            pltpu.VMEM((16, B, B), F32),
            pltpu.VMEM((16, B), F32),
            pltpu.VMEM((4, 8, 2 * B, 4 * B), F32),
            pltpu.VMEM((4, 8, 2 * B, 4 * B), F32),
            pltpu.VMEM((4, 8, 4 * B), F32),
            pltpu.VMEM((4, 8, 4 * B), F32),
            pltpu.VMEM((4, 8, 4 * B), F32),
            pltpu.VMEM((4, 8, B), F32),
            pltpu.VMEM((4, 16, 8, B), F32),
            pltpu.VMEM((4, 4, B), F32),
            pltpu.VMEM((4, 4, B), F32),
            pltpu.VMEM((4, B, 4 * B), F32),
            pltpu.VMEM((8, 2, B, B), F32),
            pltpu.VMEM((2, 2, B, B), F32),
            pltpu.VMEM((8, 2, B, B), BF16),
            pltpu.VMEM((8, 2, B, B), BF16),
            pltpu.VMEM((8, 2, B, B), BF16),
            pltpu.VMEM((8, 2, B, B), BF16),
            pltpu.VMEM((16, B, B), BF16),
            pltpu.VMEM((16, B, B), BF16),
            dma((5,)),
            dma((70,)), dma((70,)),
            dma((4, 15)), dma((4, 15)),
            dma((8,)), dma((8,)),
            dma((8,)), dma((8,)),
            dma((15,)), dma((15,)),
        ],
        compiler_params=pltpu.CompilerParams(
            collective_id=0, has_side_effects=True, vmem_limit_bytes=60 * 1024 * 1024
        ),
        name="attention_backward",
    )(queries, key_rows, value_rows, grad_output, positions.reshape(-1, B))
    return grads[0], grads[1], grads[2]


def solution(mesh):
    spec = P(("row", "col"), None)
    return jax.shard_map(
        body,
        mesh=mesh,
        in_specs=(spec, spec, spec, spec, P()),
        out_specs=(spec, spec, spec),
        check_vma=False,
    )
```

time: 64.6 us -> 59.3 us (0.918)
  Pallas kernels: 60.9 us -> 57 us
  local copies, waits for them, and re-layouts: 2.77 us -> 1.43 us
    pallas_call x1, Pallas kernels: 60.9 us -> 57 us  [body(): pl.pallas_call(kernel, out_shape=jax.ShapeDtypeStruct((3, B, B), BF16), i...]
    unnamed x7 -> x0, local copies, waits for them, and re-layouts: 2.77 us -> none
    squeeze x0 -> x1, local copies, waits for them, and re-layouts: none -> 1.43 us  [body(): return (grads[0], grads[1], grads[2])]
where the time goes in v2:
time: 59.3 us; the launch traced here: 59.1 us
  Pallas kernels  57 us (96%)
  local copies, waits for them, and re-layouts  1.43 us (2%)
  between operations  0.64 us (1%)
    pallas_call x1, Pallas kernels, body(): pl.pallas_call(kernel, out_shape=jax.ShapeDtypeStruct((3, B, B), BF16), i...  57 us
    squeeze x1, local copies, waits for them, and re-layouts, body(): return (grads[0], grads[1], grads[2])  1.43 us

profile of v2, /device:TPU:1, one launch (start us, length us, event | category | flops | bytes accessed | tf_op | source)
XLA Modules:
  0.0 59.1 jit_solution(14367595282232569549)
XLA Ops:
  0.6 57.0 %attention_backward.1 = bf16[3,128,128]{2,1,0:T(8,128)(2,1)} custom-call(bf16[128,128]{1,0:T(8,128)(2,1)} %q_ref.1, bf16[128,128]{1,0:T(8,128)(2,1)} %k_ref.1, bf16[128,128]{1,0:T(8,128)(2,1)} %v_ref.1, bf16[128,128]{1,0:T(8,128)(2,1)} %g_ref.1, s32[256,128]{1,0:T(8,128)} %bitcast.7), custom_call_target="tpu_custom_call" | custom-call | tf_op jit(solution)/shard_map/attention_backward/pallas_call | solution.py:368
  57.7 1.4 %slice_bitcast_fusion = (bf16[128,128]{1,0:T(8,128)(2,1)}, bf16[128,128]{1,0:T(8,128)(2,1)}, bf16[128,128]{1,0:T(8,128)(2,1)}) fusion(bf16[3,128,128]{2,1,0:T(8,128)(2,1)} %attention_backward.1), kind=kLoop, calls=%fused_computation | loop fusion | bytes 196608 | tf_op jit(solution)/shard_map/squeeze | solution.py:409

commit v3 on v2

v3 whole, which is shorter than its diff:
```python
import math

import jax
import jax.numpy as jnp
from jax import lax
from jax.experimental import pallas as pl
from jax.experimental.pallas import tpu as pltpu
from jax.sharding import PartitionSpec as P

MESH = pl.DeviceIdType.MESH
F32 = jnp.float32
BF16 = jnp.bfloat16
B = 128
NEG = -1e30
FLOOR = -1e6
LOG2E = math.log2(math.e)


def device(x, y, z, c):
    return (y * 2 + lax.rem(z, 2), (x * 4 + lax.div(z, 2)) * 2 + c)


def nt(a, b):
    return lax.dot_general(a, b, (((1,), (1,)), ((), ())), preferred_element_type=F32)


def nn(a, b):
    return jnp.dot(a, b, preferred_element_type=F32)


def kernel(
    q_ref, k_ref, v_ref, g_ref, pos_hbm, out_ref,
    qb, gb, kb, vb, pos_ref, ktb, posk, posq, s_buf, dp_buf, mt, zt, dt, stat_out, stat_in, factor, tops,
    w_buf, e_buf, q_scaled, g_scaled, part, tmp, pair_out, pair_in, z_out, z_in, q_out, q_in,
    ins, gs, gr, ss, sr, ps, pr, zs, zr, qs_sem, qr_sem,
):
    row, col = lax.axis_index("row"), lax.axis_index("col")
    y, zlo = lax.div(row, 2), lax.rem(row, 2)
    x, c = lax.div(col, 8), lax.rem(col, 2)
    z = lax.rem(lax.div(col, 2), 4) * 2 + zlo
    up4 = lambda a, d: lax.rem(a + d, 4)
    up8 = lambda a, d: lax.rem(a + d, 8)
    other = 1 - c
    mine = x * 4 + y
    chip_scale = LOG2E / math.sqrt(B)

    here_k = z * 2 + c
    fetch = [
        pltpu.make_async_copy(src, dst, ins.at[n])
        for n, (src, dst) in enumerate(
            ((k_ref, kb.at[here_k]), (v_ref, vb.at[here_k]), (q_ref, qb.at[mine]), (g_ref, gb.at[mine]), (pos_hbm, pos_ref))
        )
    ]
    for copy in fetch:
        copy.start()

    plane = [lax.rem(mine + d, 16) for d in range(1, 16)]
    plane_dev = [device(lax.div(s, 4), lax.rem(s, 4), z, c) for s in plane]
    barrier = pltpu.get_barrier_semaphore()
    peers = [device(up4(x, d), y, z, c) for d in (2, 1, 3)] + [device(x, up4(y, d), z, c) for d in (2, 1, 3)]
    peers += [device(x, y, up8(z, d), c) for d in (2, 6, 1, 7)] + [device(x, y, z, other)]
    for p in peers:
        pl.semaphore_signal(barrier, inc=1, device_id=p, device_id_type=MESH)
    for copy in fetch[:4]:
        copy.wait()
    pl.semaphore_wait(barrier, len(peers))

    sent = []

    def send(src, dst, send_sem, recv_sem, to):
        copy = pltpu.make_async_remote_copy(
            src_ref=src, dst_ref=dst, send_sem=send_sem, recv_sem=recv_sem, device_id=to, device_id_type=MESH
        )
        copy.start()
        sent.append(copy)
        return copy

    count = [0]

    def gsend(src, dst, to):
        i = count[0]
        count[0] += 1
        return send(src, dst, gs.at[i], gr.at[i], to)

    slot = lambda a, b: a * 4 + b
    xr, xl, yr, yl = up4(x, 1), up4(x, 3), up4(y, 1), up4(y, 3)
    x2, y2 = up4(x, 2), up4(y, 2)
    to_xr, to_xl = device(xr, y, z, c), device(xl, y, z, c)
    to_yr, to_yl = device(x, yr, z, c), device(x, yl, z, c)
    to_pair = device(x, y, z, other)

    done = set()

    def need(*copies):
        for copy in copies:
            if id(copy) not in done:
                done.add(id(copy))
                copy.wait_recv()

    to_x2, to_y2 = device(x2, y, z, c), device(x, y2, z, c)
    plans = (
        ({}, qb, lambda i, j: slot(i, j), x, y, (xl, xr, x2), (to_xr, to_xl, to_x2), (to_yr, to_yl, to_y2)),
        ({}, gb, lambda i, j: slot(j, i), y, x, (yl, yr, y2), (to_yr, to_yl, to_y2), (to_xr, to_xl, to_x2)),
    )
    kv = (kb, vb)
    kslot = lambda zz, cc: zz * 2 + cc
    along, pair = {}, {}

    def send_z(w, off, *steps):
        src = kv[w].at[kslot(up8(z, off), c)]
        for d in steps:
            along[w, (off - d) % 8] = gsend(src, src, device(x, y, up8(z, d), c))

    def send_pair(off):
        for w in range(2):
            if off:
                need(along[w, off])
            src = kv[w].at[kslot(up8(z, off), c)]
            pair[w, off] = gsend(src, src, to_pair)

    for w in range(2):
        send_z(w, 0, 2, 6)
    for st, buf, at, a, b, ias, to_a, to_b in plans:
        src = buf.at[at(a, b)]
        for n in (2, 0, 1):
            st["a", n] = gsend(src, src, to_a[n])
        for n in (2, 0, 1):
            st["b", 3, n] = gsend(src, src, to_b[n])
    for w in range(2):
        send_z(w, 0, 1, 7)
    send_pair(0)

    fetch[4].wait()
    zhi_col = lax.div(z, 2) * 2 + c
    for s in range(16):
        i, j = s // 4, s % 4
        posq[pl.ds(s, 1), :] = pos_ref[pl.ds((j * 2 + zlo) * 32 + i * 8 + zhi_col, 1), :].astype(F32)
    for s in range(16):
        zz, cc = s // 2, s % 2
        line = pos_ref[pl.ds((y * 2 + zz % 2) * 32 + (x * 4 + zz // 2) * 2 + cc, 1), :].astype(F32)
        posk[s] = jnp.broadcast_to(line, (B, B)).T

    def tile(t, zz):
        q_tile = qb[pl.ds(4 * t, 4)].reshape(4 * B, B)
        g_tile = gb[pl.ds(4 * t, 4)].reshape(4 * B, B)
        k_tile = kb[pl.ds(2 * zz, 2)].reshape(2 * B, B)
        v_tile = vb[pl.ds(2 * zz, 2)].reshape(2 * B, B)
        pq = jnp.concatenate([posq[pl.ds(4 * t + j, 1), :] for j in range(4)], axis=1)
        pk = posk[pl.ds(2 * zz, 2)].reshape(2 * B, B)
        pk = jnp.concatenate([pk] * 4, axis=1)
        s = jnp.where(pq >= pk, nt(k_tile, q_tile) * chip_scale, NEG)
        s_buf[t, zz] = s
        m = jnp.maximum(jnp.max(s, axis=0, keepdims=True), FLOOR)
        dp = nt(v_tile, g_tile)
        dp_buf[t, zz] = dp
        w = jnp.exp2(s - m)
        mt[t, pl.ds(zz, 1), :] = m
        zt[t, pl.ds(zz, 1), :] = jnp.sum(w, axis=0, keepdims=True)
        dt[t, pl.ds(zz, 1), :] = jnp.sum(w * dp, axis=0, keepdims=True)

    def tiles(n, pick):
        def step(i, carry):
            for t, zz in pick(i):
                tile(t, zz)
            return carry

        lax.fori_loop(0, n, step, 0)

    near = lambda i: up8(z, i + 5 * lax.div(i, 2))
    both = lambda i, d: up8(z, d + i * (8 - 2 * d))

    for n in range(2):
        for st, buf, at, a, b, ias, to_a, to_b in plans:
            need(st["a", n])
            src = buf.at[at(ias[n], b)]
            for m in (2, 0, 1):
                st["b", n, m] = gsend(src, src, to_b[m])
    for w in range(2):
        need(along[w, 6])
        send_z(w, 6, *((2, 1) if w == 0 else (1,)))
        need(along[w, 2])
        send_z(w, 2, *((6, 7) if w == 1 else (7,)))
    for st, buf, at, a, b, ias, to_a, to_b in plans:
        need(st["a", 2])
        src = buf.at[at(ias[2], b)]
        for m in (2, 0, 1):
            st["b", 2, m] = gsend(src, src, to_b[m])
    for off in (1, 7, 2, 6):
        send_pair(off)
    sq, sg = plans[0][0], plans[1][0]

    def need_column(n):
        need(*(sq["b", n, m] for m in range(3)))
        if n < 3:
            need(*(sg["b", m, n] for m in range(4)))

    need_column(3)
    need(*(pair[w, off] for w in range(2) for off in (0, 1, 7)))
    tiles(3, lambda i: [(x, near(i))])
    need(*(pair[w, off] for w in range(2) for off in (2, 6)))
    tiles(1, lambda i: [(x, both(0, 2)), (x, both(1, 2))])
    need_column(0)
    need_column(1)
    tiles(3, lambda i: [(xl, near(i)), (xr, near(i))])
    for off in (3, 5, 4):
        send_pair(off)
    tiles(2, lambda i: [(xl, both(i, 2)), (xr, both(i, 2))])
    need_column(2)
    tiles(3, lambda i: [(x2, near(i))])
    tiles(1, lambda i: [(x2, both(0, 2)), (x2, both(1, 2))])
    need(*(pair[w, off] for w in range(2) for off in (3, 5)))
    tiles(4, lambda i: [(i, both(0, 3)), (i, both(1, 3))])
    need(*(pair[w, 4] for w in range(2)))

    def finish(t, carry):
        tile(t, up8(z, 4))
        maxes = mt[t]
        top = jnp.max(maxes, axis=0, keepdims=True)
        tops[t, 0:1, :] = top
        f = jnp.exp2(maxes - top)
        total = jnp.sum(zt[t] * f, axis=0, keepdims=True)
        dot = jnp.sum(dt[t] * f, axis=0, keepdims=True)
        some = total > 0.0
        safe = jnp.where(some, total, 1.0)
        level = jnp.where(some, top + jnp.log(safe) * LOG2E, NEG)
        mean = dot / safe
        tops[t, 1:2, :] = mean
        for j in range(4):
            stat_out[t, pl.ds(j, 1), :] = level[:, j * B : (j + 1) * B]
            stat_out[t, pl.ds(4 + j, 1), :] = mean[:, j * B : (j + 1) * B]
        stat_in[t, mine] = stat_out[t]
        for d in range(15):
            pltpu.make_async_remote_copy(
                src_ref=stat_out.at[t], dst_ref=stat_in.at[t, mine], send_sem=ss.at[t, d], recv_sem=sr.at[t, d],
                device_id=plane_dev[d], device_id_type=MESH,
            ).start()
        return carry

    lax.fori_loop(0, 4, finish, 0)

    for zz in range(8):
        ktb[zz] = kb[pl.ds(2 * zz, 2)].reshape(2 * B, B).T

    def weigh(t, carry):
        top, mean = tops[t, 0:1, :], tops[t, 1:2, :]

        def step(i, carry):
            for zz in (2 * i, 2 * i + 1):
                w = jnp.exp2(s_buf[t, zz] - top)
                w_buf[t, zz] = w.astype(BF16)
                e_buf[t, zz] = (w * (dp_buf[t, zz] - mean)).astype(BF16)
            return carry

        return lax.fori_loop(0, 4, step, carry)

    lax.fori_loop(0, 4, weigh, 0)

    def combine(t, carry):
        for d in range(15):
            copy = pltpu.make_async_remote_copy(
                src_ref=stat_out.at[t], dst_ref=stat_in.at[t, lax.rem(mine + 15 - d, 16)], send_sem=ss.at[t, d],
                recv_sem=sr.at[t, d], device_id=plane_dev[d], device_id_type=MESH,
            )
            copy.wait_recv()
            copy.wait_send()
        level = stat_in[t, :, 0:4, :]
        mean = stat_in[t, :, 4:8, :]
        top = jnp.max(level, axis=0)
        e = jnp.exp2(level - top[None])
        total = jnp.sum(e, axis=0)
        lse = top + jnp.log(total) * LOG2E
        delta = jnp.sum(e * mean, axis=0) / total
        for j in range(4):
            here = slice(j * B, (j + 1) * B)
            f = jnp.exp2(tops[t, 0:1, here] - lse[j : j + 1])
            h = (tops[t, 1:2, here] - delta[j : j + 1]) * f
            factor[0, pl.ds(4 * t + j, 1), :] = f
            factor[1, pl.ds(4 * t + j, 1), :] = h
        return carry

    lax.fori_loop(0, 4, combine, 0)

    column = lambda i: up4(x, (2, 1, 3, 0)[i])

    def q_copy(i, j):
        return pltpu.make_async_remote_copy(
            src_ref=q_out.at[i, up4(y, j)], dst_ref=q_in.at[i, j], send_sem=qs_sem.at[i, j], recv_sem=qr_sem.at[i, j],
            device_id=device(column(i), up4(y, j), z, c), device_id_type=MESH,
        )

    def query_side(i):
        t = column(i)
        of_e = nn(ktb[0], e_buf[t, 0])
        of_w = nn(ktb[0], w_buf[t, 0])
        for zz in range(1, 8):
            of_e += nn(ktb[zz], e_buf[t, zz])
            of_w += nn(ktb[zz], w_buf[t, zz])
        for j in range(4):
            here = slice(j * B, (j + 1) * B)
            f = factor[0, pl.ds(4 * t + j, 1), :]
            h = factor[1, pl.ds(4 * t + j, 1), :]
            q_out[i, j] = (of_e[:, here] * f + of_w[:, here] * h).astype(BF16)
        for j in (2, 1, 3, 0):
            if (i, j) != (3, 0):
                q_copy(i, j).start()

    f_col, h_col = factor[0].T, factor[1].T
    for s in range(16):
        f, h = f_col[:, s : s + 1], h_col[:, s : s + 1]
        rows = qb[s].astype(F32)
        q_scaled[s] = (rows * f).astype(BF16)
        g_scaled[s, :, :B] = (gb[s].astype(F32) * f).astype(BF16)
        g_scaled[s, :, B:] = (rows * h).astype(BF16)

    def pair_copy(off):
        return pltpu.make_async_remote_copy(
            src_ref=pair_out.at[off], dst_ref=pair_in.at[off], send_sem=ps.at[off], recv_sem=pr.at[off],
            device_id=to_pair, device_id_type=MESH,
        )

    to_z = lambda d: device(x, y, up8(z, d), c)

    def z_copy(n, src, dst, d):
        return pltpu.make_async_remote_copy(
            src_ref=src, dst_ref=dst, send_sem=zs.at[n], recv_sem=zr.at[n], device_id=to_z(d), device_id_type=MESH
        )

    hops = {
        4: (z_copy(0, z_out.at[4, 0], z_in.at[0, 0], 2), z_copy(1, z_out.at[4, 1], z_in.at[0, 1], 6)),
        3: (z_copy(2, z_out.at[3], z_in.at[1], 1),),
        5: (z_copy(3, z_out.at[5], z_in.at[2], 7),),
        2: (z_copy(4, z_out.at[2], z_in.at[3], 2),),
        6: (z_copy(5, z_out.at[6], z_in.at[4], 6),),
        1: (z_copy(6, z_out.at[1], z_in.at[5], 1),),
        7: (z_copy(7, z_out.at[7], z_in.at[6], 7),),
    }

    def pass_on(off):
        pair_copy(off).wait_recv()
        for w in range(2):
            total = part[off, w] + pair_in[off, w].astype(F32)
            if off in (2, 6):
                if w == 0:
                    hops[3 if off == 2 else 5][0].wait_recv()
                total += z_in[1 if off == 2 else 2, w].astype(F32)
                if w == (0 if off == 2 else 1):
                    hops[4][w].wait_recv()
                    total += z_in[0, w].astype(F32)
            z_out[off, w] = total.astype(BF16)
        for copy in hops[off]:
            copy.start()

    def key_side(off):
        zz = up8(z, off)
        dk = jnp.zeros((2 * B, B), F32)
        dvk = jnp.zeros((2 * B, 2 * B), F32)
        for t in range(4):
            dk += nn(e_buf[t, zz], q_scaled[4 * t : 4 * t + 4].reshape(4 * B, B))
            dvk += nn(w_buf[t, zz], g_scaled[4 * t : 4 * t + 4].reshape(4 * B, 2 * B))
        for w, total in enumerate((dk + dvk[:, B:], dvk[:, :B])):
            tmp[w] = total.reshape(2, B, B)
            part[off, w] = tmp[w, c]
            pair_out[off, w] = tmp[w, other].astype(BF16)
        pair_copy(off).start()

    key_side(4)
    key_side(3)
    pass_on(4)
    key_side(5)
    pass_on(3)
    query_side(0)
    pass_on(5)
    key_side(2)
    key_side(6)
    query_side(1)
    pass_on(2)
    query_side(2)
    query_side(3)
    pass_on(6)
    key_side(1)
    key_side(7)
    pass_on(1)
    key_side(0)
    pass_on(7)

    scale = 1.0 / math.sqrt(B)
    own = q_out[3, y].astype(F32)
    for i in range(4):
        for j in range(4):
            if (i, j) != (3, 0):
                q_copy(i, j).wait_recv()
                own += q_in[i, j].astype(F32)
    out_ref[0] = (own * scale).T.astype(BF16)

    pair_copy(0).wait_recv()
    acc = [part[0, w] + pair_in[0, w].astype(F32) for w in range(2)]
    for off, n in ((2, 3), (6, 4), (1, 5), (7, 6)):
        hops[off][0].wait_recv()
        for w in range(2):
            acc[w] += z_in[n, w].astype(F32)
    out_ref[1] = (acc[0] * scale).astype(BF16)
    out_ref[2] = acc[1].astype(BF16)

    for copy in sent:
        copy.wait_send()
    for off in range(8):
        pair_copy(off).wait_send()
        for copy in hops.get(off, ()):
            copy.wait_send()
    for i in range(4):
        for j in range(4):
            if (i, j) != (3, 0):
                q_copy(i, j).wait_send()


def body(queries, key_rows, value_rows, grad_output, positions):
    vmem = pl.BlockSpec(memory_space=pltpu.VMEM)
    hbm = pl.BlockSpec(memory_space=pl.ANY)
    dma = pltpu.SemaphoreType.DMA
    blocks = pltpu.VMEM((16, B, B), BF16)
    grads = pl.pallas_call(
        kernel,
        out_shape=jax.ShapeDtypeStruct((3, B, B), BF16),
        in_specs=[hbm] * 5,
        out_specs=vmem,
        scratch_shapes=[
            blocks, blocks, blocks, blocks,
            pltpu.VMEM((256, B), jnp.int32),
            pltpu.VMEM((8, B, 2 * B), BF16),
            pltpu.VMEM((16, B, B), F32),
            pltpu.VMEM((16, B), F32),
            pltpu.VMEM((4, 8, 2 * B, 4 * B), F32),
            pltpu.VMEM((4, 8, 2 * B, 4 * B), F32),
            pltpu.VMEM((4, 8, 4 * B), F32),
            pltpu.VMEM((4, 8, 4 * B), F32),
            pltpu.VMEM((4, 8, 4 * B), F32),
            pltpu.VMEM((4, 8, B), F32),
            pltpu.VMEM((4, 16, 8, B), F32),
            pltpu.VMEM((2, 16, B), F32),
            pltpu.VMEM((4, 8, 4 * B), F32),
            pltpu.VMEM((4, 8, 2 * B, 4 * B), BF16),
            pltpu.VMEM((4, 8, 2 * B, 4 * B), BF16),
            pltpu.VMEM((16, B, B), BF16),
            pltpu.VMEM((16, B, 2 * B), BF16),
            pltpu.VMEM((8, 2, B, B), F32),
            pltpu.VMEM((2, 2, B, B), F32),
            pltpu.VMEM((8, 2, B, B), BF16),
            pltpu.VMEM((8, 2, B, B), BF16),
            pltpu.VMEM((8, 2, B, B), BF16),
            pltpu.VMEM((7, 2, B, B), BF16),
            pltpu.VMEM((4, 4, B, B), BF16),
            pltpu.VMEM((4, 4, B, B), BF16),
            dma((5,)),
            dma((60,)), dma((60,)),
            dma((4, 15)), dma((4, 15)),
            dma((8,)), dma((8,)),
            dma((8,)), dma((8,)),
            dma((4, 4)), dma((4, 4)),
        ],
        compiler_params=pltpu.CompilerParams(
            collective_id=0, has_side_effects=True, vmem_limit_bytes=63 * 1024 * 1024
        ),
        name="attention_backward",
    )(queries, key_rows, value_rows, grad_output, positions.reshape(-1, B))
    return grads[0], grads[1], grads[2]


def solution(mesh):
    spec = P(("row", "col"), None)
    return jax.shard_map(
        body,
        mesh=mesh,
        in_specs=(spec, spec, spec, spec, P()),
        out_specs=(spec, spec, spec),
        check_vma=False,
    )
```

time: 59.3 us -> 56.1 us (0.946)
  Pallas kernels: 57 us -> 53.8 us
    pallas_call x1, Pallas kernels: 57 us -> 53.8 us  [body(): pl.pallas_call(kernel, out_shape=jax.ShapeDtypeStruct((3, B, B), BF16), i...]
where the time goes in v3:
time: 56.1 us; the launch traced here: 55.9 us
  Pallas kernels  53.8 us (96%)
  local copies, waits for them, and re-layouts  1.43 us (3%)
  between operations  0.64 us (1%)
    pallas_call x1, Pallas kernels, body(): pl.pallas_call(kernel, out_shape=jax.ShapeDtypeStruct((3, B, B), BF16), i...  53.8 us
    squeeze x1, local copies, waits for them, and re-layouts, body(): return (grads[0], grads[1], grads[2])  1.43 us

profile of v3, /device:TPU:1, one launch (start us, length us, event | category | flops | bytes accessed | tf_op | source)
XLA Modules:
  0.0 55.9 jit_solution(6369309676262240423)
XLA Ops:
  0.6 53.8 %attention_backward.1 = bf16[3,128,128]{2,1,0:T(8,128)(2,1)} custom-call(bf16[128,128]{1,0:T(8,128)(2,1)} %q_ref.1, bf16[128,128]{1,0:T(8,128)(2,1)} %k_ref.1, bf16[128,128]{1,0:T(8,128)(2,1)} %v_ref.1, bf16[128,128]{1,0:T(8,128)(2,1)} %g_ref.1, s32[256,128]{1,0:T(8,128)} %bitcast.7), custom_call_target="tpu_custom_call" | custom-call | tf_op jit(solution)/shard_map/attention_backward/pallas_call | solution.py:421
  54.5 1.4 %slice_bitcast_fusion = (bf16[128,128]{1,0:T(8,128)(2,1)}, bf16[128,128]{1,0:T(8,128)(2,1)}, bf16[128,128]{1,0:T(8,128)(2,1)}) fusion(bf16[3,128,128]{2,1,0:T(8,128)(2,1)} %attention_backward.1), kind=kLoop, calls=%fused_computation | loop fusion | bytes 196608 | tf_op jit(solution)/shard_map/squeeze | solution.py:465

commit v4 on v3

--- a/solution.py
+++ b/solution.py
@@ -30,7 +30,7 @@
 
 def kernel(
     q_ref, k_ref, v_ref, g_ref, pos_hbm, out_ref,
-    qb, gb, kb, vb, pos_ref, ktb, posk, posq, s_buf, dp_buf, mt, zt, dt, stat_out, stat_in, factor, tops,
+    qb, gb, kvb, pos_ref, ktb, posk, posq, s_buf, dp_buf, mt, zt, dt, stat_out, stat_in, factor, tops,
     w_buf, e_buf, q_scaled, g_scaled, part, tmp, pair_out, pair_in, z_out, z_in, q_out, q_in,
     ins, gs, gr, ss, sr, ps, pr, zs, zr, qs_sem, qr_sem,
 ):
@@ -47,8 +47,14 @@
     here_k = z * 2 + c
     fetch = [
         pltpu.make_async_copy(src, dst, ins.at[n])
-        for n, (src, dst) in enumerate(
-            ((k_ref, kb.at[here_k]), (v_ref, vb.at[here_k]), (q_ref, qb.at[mine]), (g_ref, gb.at[mine]), (pos_hbm, pos_ref))
+        for src, dst, n in (
+            (
+                (k_ref, kvb.at[here_k, 0], 0),
+                (v_ref, kvb.at[here_k, 1], 0),
+                (q_ref, qb.at[mine], 0),
+                (g_ref, gb.at[mine], 0),
+                (pos_hbm, pos_ref, 1),
+            )
         )
     ]
     for copy in fetch:
@@ -61,73 +67,67 @@
     peers += [device(x, y, up8(z, d), c) for d in (2, 6, 1, 7)] + [device(x, y, z, other)]
     for p in peers:
         pl.semaphore_signal(barrier, inc=1, device_id=p, device_id_type=MESH)
-    for copy in fetch[:4]:
-        copy.wait()
+    pltpu.make_async_copy(qb.at[0:4], qb.at[0:4], ins.at[0]).wait()
     pl.semaphore_wait(barrier, len(peers))
 
-    sent = []
-
-    def send(src, dst, send_sem, recv_sem, to):
-        copy = pltpu.make_async_remote_copy(
-            src_ref=src, dst_ref=dst, send_sem=send_sem, recv_sem=recv_sem, device_id=to, device_id_type=MESH
+    to_pair = device(x, y, z, other)
+
+    def whole(ref, send_sem, recv_sem):
+        return pltpu.make_async_remote_copy(
+            src_ref=ref, dst_ref=ref, send_sem=send_sem, recv_sem=recv_sem, device_id=to_pair, device_id_type=MESH
         )
-        copy.start()
-        sent.append(copy)
-        return copy
-
-    count = [0]
-
-    def gsend(src, dst, to):
-        i = count[0]
-        count[0] += 1
-        return send(src, dst, gs.at[i], gr.at[i], to)
+
+    def send(src, to, n):
+        pltpu.make_async_remote_copy(
+            src_ref=src, dst_ref=src, send_sem=gs.at[0], recv_sem=gr.at[n], device_id=to, device_id_type=MESH
+        ).start()
+
+    done = set()
+
+    def need(n, ref):
+        if n not in done:
+            done.add(n)
+            whole(ref, gs.at[0], gr.at[n]).wait_recv()
 
     slot = lambda a, b: a * 4 + b
     xr, xl, yr, yl = up4(x, 1), up4(x, 3), up4(y, 1), up4(y, 3)
     x2, y2 = up4(x, 2), up4(y, 2)
     to_xr, to_xl = device(xr, y, z, c), device(xl, y, z, c)
     to_yr, to_yl = device(x, yr, z, c), device(x, yl, z, c)
-    to_pair = device(x, y, z, other)
-
-    done = set()
-
-    def need(*copies):
-        for copy in copies:
-            if id(copy) not in done:
-                done.add(id(copy))
-                copy.wait_recv()
-
     to_x2, to_y2 = device(x2, y, z, c), device(x, y2, z, c)
     plans = (
-        ({}, qb, lambda i, j: slot(i, j), x, y, (xl, xr, x2), (to_xr, to_xl, to_x2), (to_yr, to_yl, to_y2)),
-        ({}, gb, lambda i, j: slot(j, i), y, x, (yl, yr, y2), (to_yr, to_yl, to_y2), (to_xr, to_xl, to_x2)),
+        (16, qb, lambda i, j: slot(i, j), x, y, (xl, xr, x2), (to_xr, to_xl, to_x2), (to_yr, to_yl, to_y2)),
+        (19, gb, lambda i, j: slot(j, i), y, x, (yl, yr, y2), (to_yr, to_yl, to_y2), (to_xr, to_xl, to_x2)),
     )
-    kv = (kb, vb)
-    kslot = lambda zz, cc: zz * 2 + cc
-    along, pair = {}, {}
-
-    def send_z(w, off, *steps):
-        src = kv[w].at[kslot(up8(z, off), c)]
-        for d in steps:
-            along[w, (off - d) % 8] = gsend(src, src, device(x, y, up8(z, d), c))
+    kv_at = lambda off: kvb.at[up8(z, off) * 2 + c]
+    up = lambda d: device(x, y, up8(z, d), c)
+
+    def send_across(p, n, src):
+        to_b = plans[p][-1]
+        for m in (2, 0, 1):
+            send(src, to_b[m], 22 + (n if p == 0 else m))
 
     def send_pair(off):
-        for w in range(2):
-            if off:
-                need(along[w, off])
-            src = kv[w].at[kslot(up8(z, off), c)]
-            pair[w, off] = gsend(src, src, to_pair)
-
-    for w in range(2):
-        send_z(w, 0, 2, 6)
-    for st, buf, at, a, b, ias, to_a, to_b in plans:
+        if off == 4:
+            need(4, kv_at(4).at[0])
+            need(0, kv_at(4).at[1])
+        elif off:
+            need(off, kv_at(off))
+        send(kv_at(off), to_pair, 8 + off)
+
+    def need_pair(*offs):
+        for off in offs:
+            need(8 + off, kv_at(off))
+
+    send(kv_at(0), up(2), 6)
+    send(kv_at(0), up(6), 2)
+    for p, (first, buf, at, a, b, ias, to_a, to_b) in enumerate(plans):
         src = buf.at[at(a, b)]
         for n in (2, 0, 1):
-            st["a", n] = gsend(src, src, to_a[n])
-        for n in (2, 0, 1):
-            st["b", 3, n] = gsend(src, src, to_b[n])
-    for w in range(2):
-        send_z(w, 0, 1, 7)
+            send(src, to_a[n], first + n)
+        send_across(p, 3, src)
+    send(kv_at(0), up(1), 7)
+    send(kv_at(0), up(7), 1)
     send_pair(0)
 
     fetch[4].wait()
@@ -143,8 +143,8 @@
     def tile(t, zz):
         q_tile = qb[pl.ds(4 * t, 4)].reshape(4 * B, B)
         g_tile = gb[pl.ds(4 * t, 4)].reshape(4 * B, B)
-        k_tile = kb[pl.ds(2 * zz, 2)].reshape(2 * B, B)
-        v_tile = vb[pl.ds(2 * zz, 2)].reshape(2 * B, B)
+        k_tile = kvb[pl.ds(2 * zz, 2), 0].reshape(2 * B, B)
+        v_tile = kvb[pl.ds(2 * zz, 2), 1].reshape(2 * B, B)
         pq = jnp.concatenate([posq[pl.ds(4 * t + j, 1), :] for j in range(4)], axis=1)
         pk = posk[pl.ds(2 * zz, 2)].reshape(2 * B, B)
         pk = jnp.concatenate([pk] * 4, axis=1)
@@ -169,35 +169,31 @@
     near = lambda i: up8(z, i + 5 * lax.div(i, 2))
     both = lambda i, d: up8(z, d + i * (8 - 2 * d))
 
-    for n in range(2):
-        for st, buf, at, a, b, ias, to_a, to_b in plans:
-            need(st["a", n])
+    def across(n):
+        for p, (first, buf, at, a, b, ias, to_a, to_b) in enumerate(plans):
             src = buf.at[at(ias[n], b)]
-            for m in (2, 0, 1):
-                st["b", n, m] = gsend(src, src, to_b[m])
-    for w in range(2):
-        need(along[w, 6])
-        send_z(w, 6, *((2, 1) if w == 0 else (1,)))
-        need(along[w, 2])
-        send_z(w, 2, *((6, 7) if w == 1 else (7,)))
-    for st, buf, at, a, b, ias, to_a, to_b in plans:
-        need(st["a", 2])
-        src = buf.at[at(ias[2], b)]
-        for m in (2, 0, 1):
-            st["b", 2, m] = gsend(src, src, to_b[m])
+            need(first + n, src)
+            send_across(p, n, src)
+
+    across(0)
+    across(1)
+    need(6, kv_at(6))
+    send(kv_at(6).at[0], up(2), 4)
+    send(kv_at(6), up(1), 5)
+    need(2, kv_at(2))
+    send(kv_at(2).at[1], up(6), 0)
+    send(kv_at(2), up(7), 3)
+    across(2)
     for off in (1, 7, 2, 6):
         send_pair(off)
-    sq, sg = plans[0][0], plans[1][0]
 
     def need_column(n):
-        need(*(sq["b", n, m] for m in range(3)))
-        if n < 3:
-            need(*(sg["b", m, n] for m in range(4)))
+        need(22 + n, qb.at[0 : 7 if n < 3 else 3])
 
     need_column(3)
-    need(*(pair[w, off] for w in range(2) for off in (0, 1, 7)))
+    need_pair(0, 1, 7)
     tiles(3, lambda i: [(x, near(i))])
-    need(*(pair[w, off] for w in range(2) for off in (2, 6)))
+    need_pair(2, 6)
     tiles(1, lambda i: [(x, both(0, 2)), (x, both(1, 2))])
     need_column(0)
     need_column(1)
@@ -208,9 +204,9 @@
     need_column(2)
     tiles(3, lambda i: [(x2, near(i))])
     tiles(1, lambda i: [(x2, both(0, 2)), (x2, both(1, 2))])
-    need(*(pair[w, off] for w in range(2) for off in (3, 5)))
+    need_pair(3, 5)
     tiles(4, lambda i: [(i, both(0, 3)), (i, both(1, 3))])
-    need(*(pair[w, 4] for w in range(2)))
+    need_pair(4)
 
     def finish(t, carry):
         tile(t, up8(z, 4))
@@ -231,7 +227,7 @@
         stat_in[t, mine] = stat_out[t]
         for d in range(15):
             pltpu.make_async_remote_copy(
-                src_ref=stat_out.at[t], dst_ref=stat_in.at[t, mine], send_sem=ss.at[t, d], recv_sem=sr.at[t, d],
+                src_ref=stat_out.at[t], dst_ref=stat_in.at[t, mine], send_sem=ss.at[0], recv_sem=sr.at[t],
                 device_id=plane_dev[d], device_id_type=MESH,
             ).start()
         return carry
@@ -239,7 +235,7 @@
     lax.fori_loop(0, 4, finish, 0)
 
     for zz in range(8):
-        ktb[zz] = kb[pl.ds(2 * zz, 2)].reshape(2 * B, B).T
+        ktb[zz] = kvb[pl.ds(2 * zz, 2), 0].reshape(2 * B, B).T
 
     def weigh(t, carry):
         top, mean = tops[t, 0:1, :], tops[t, 1:2, :]
@@ -256,13 +252,7 @@
     lax.fori_loop(0, 4, weigh, 0)
 
     def combine(t, carry):
-        for d in range(15):
-            copy = pltpu.make_async_remote_copy(
-                src_ref=stat_out.at[t], dst_ref=stat_in.at[t, lax.rem(mine + 15 - d, 16)], send_sem=ss.at[t, d],
-                recv_sem=sr.at[t, d], device_id=plane_dev[d], device_id_type=MESH,
-            )
-            copy.wait_recv()
-            copy.wait_send()
+        whole(stat_in.at[t, 0:15], ss.at[0], sr.at[t]).wait_recv()
         level = stat_in[t, :, 0:4, :]
         mean = stat_in[t, :, 4:8, :]
         top = jnp.max(level, axis=0)
@@ -284,7 +274,7 @@
 
     def q_copy(i, j):
         return pltpu.make_async_remote_copy(
-            src_ref=q_out.at[i, up4(y, j)], dst_ref=q_in.at[i, j], send_sem=qs_sem.at[i, j], recv_sem=qr_sem.at[i, j],
+            src_ref=q_out.at[4 * i + up4(y, j)], dst_ref=q_in.at[4 * i + j], send_sem=qs_sem.at[0], recv_sem=qr_sem.at[0],
             device_id=device(column(i), up4(y, j), z, c), device_id_type=MESH,
         )
 
@@ -299,7 +289,7 @@
             here = slice(j * B, (j + 1) * B)
             f = factor[0, pl.ds(4 * t + j, 1), :]
             h = factor[1, pl.ds(4 * t + j, 1), :]
-            q_out[i, j] = (of_e[:, here] * f + of_w[:, here] * h).astype(BF16)
+            q_out[4 * i + j] = (of_e[:, here] * f + of_w[:, here] * h).astype(BF16)
         for j in (2, 1, 3, 0):
             if (i, j) != (3, 0):
                 q_copy(i, j).start()
@@ -314,7 +304,7 @@
 
     def pair_copy(off):
         return pltpu.make_async_remote_copy(
-            src_ref=pair_out.at[off], dst_ref=pair_in.at[off], send_sem=ps.at[off], recv_sem=pr.at[off],
+            src_ref=pair_out.at[off], dst_ref=pair_in.at[off], send_sem=ps.at[0], recv_sem=pr.at[off],
             device_id=to_pair, device_id_type=MESH,
         )
 
@@ -322,7 +312,7 @@
 
     def z_copy(n, src, dst, d):
         return pltpu.make_async_remote_copy(
-            src_ref=src, dst_ref=dst, send_sem=zs.at[n], recv_sem=zr.at[n], device_id=to_z(d), device_id_type=MESH
+            src_ref=src, dst_ref=dst, send_sem=zs.at[0], recv_sem=zr.at[n], device_id=to_z(d), device_id_type=MESH
         )
 
     hops = {
@@ -365,52 +355,45 @@
 
     key_side(4)
     key_side(3)
+    key_side(5)
+    key_side(2)
     pass_on(4)
-    key_side(5)
+    key_side(6)
     pass_on(3)
     query_side(0)
     pass_on(5)
-    key_side(2)
-    key_side(6)
     query_side(1)
-    pass_on(2)
     query_side(2)
     query_side(3)
-    pass_on(6)
     key_side(1)
     key_side(7)
+    key_side(0)
+    pass_on(2)
+    pass_on(6)
     pass_on(1)
-    key_side(0)
     pass_on(7)
 
     scale = 1.0 / math.sqrt(B)
-    own = q_out[3, y].astype(F32)
-    for i in range(4):
-        for j in range(4):
-            if (i, j) != (3, 0):
-                q_copy(i, j).wait_recv()
-                own += q_in[i, j].astype(F32)
-    out_ref[0] = (own * scale).T.astype(BF16)
-
     pair_copy(0).wait_recv()
     acc = [part[0, w] + pair_in[0, w].astype(F32) for w in range(2)]
-    for off, n in ((2, 3), (6, 4), (1, 5), (7, 6)):
+    own = q_out[12 + y].astype(F32)
+    whole(q_in.at[0:15], qs_sem.at[0], qr_sem.at[0]).wait_recv()
+    for n in range(16):
+        if n != 12:
+            own += q_in[n].astype(F32)
+    out_ref[0] = (own * scale).T.astype(BF16)
+    for off, n in ((1, 5), (7, 6), (2, 3), (6, 4)):
         hops[off][0].wait_recv()
         for w in range(2):
             acc[w] += z_in[n, w].astype(F32)
     out_ref[1] = (acc[0] * scale).astype(BF16)
     out_ref[2] = acc[1].astype(BF16)
 
-    for copy in sent:
-        copy.wait_send()
-    for off in range(8):
-        pair_copy(off).wait_send()
-        for copy in hops.get(off, ()):
-            copy.wait_send()
-    for i in range(4):
-        for j in range(4):
-            if (i, j) != (3, 0):
-                q_copy(i, j).wait_send()
+    whole(s_buf.at[0, 0:5, 0:192, :], gs.at[0], gr.at[0]).wait_send()
+    whole(stat_in.at[:, 0:15], ss.at[0], sr.at[0]).wait_send()
+    whole(pair_out, ps.at[0], pr.at[0]).wait_send()
+    whole(z_out.at[1:8], zs.at[0], zr.at[0]).wait_send()
+    whole(q_in.at[0:15], qs_sem.at[0], qr_sem.at[0]).wait_send()
 
 
 def body(queries, key_rows, value_rows, grad_output, positions):
@@ -424,7 +407,8 @@
         in_specs=[hbm] * 5,
         out_specs=vmem,
         scratch_shapes=[
-            blocks, blocks, blocks, blocks,
+            blocks, blocks,
+            pltpu.VMEM((16, 2, B, B), BF16),
             pltpu.VMEM((256, B), jnp.int32),
             pltpu.VMEM((8, B, 2 * B), BF16),
             pltpu.VMEM((16, B, B), F32),
@@ -448,14 +432,13 @@
             pltpu.VMEM((8, 2, B, B), BF16),
             pltpu.VMEM((8, 2, B, B), BF16),
             pltpu.VMEM((7, 2, B, B), BF16),
-            pltpu.VMEM((4, 4, B, B), BF16),
-            pltpu.VMEM((4, 4, B, B), BF16),
-            dma((5,)),
-            dma((60,)), dma((60,)),
-            dma((4, 15)), dma((4, 15)),
-            dma((8,)), dma((8,)),
-            dma((8,)), dma((8,)),
-            dma((4, 4)), dma((4, 4)),
+            blocks, blocks,
+            dma((2,)),
+            dma((1,)), dma((26,)),
+            dma((1,)), dma((4,)),
+            dma((1,)), dma((8,)),
+            dma((1,)), dma((8,)),
+            dma((1,)), dma((1,)),
         ],
         compiler_params=pltpu.CompilerParams(
             collective_id=0, has_side_effects=True, vmem_limit_bytes=63 * 1024 * 1024

time: 56.1 us -> 53.9 us (0.961)
  Pallas kernels: 53.8 us -> 51.6 us
    pallas_call x1, Pallas kernels: 53.8 us -> 51.6 us  [body(): pl.pallas_call(kernel, out_shape=jax.ShapeDtypeStruct((3, B, B), BF16), i...]
where the time goes in v4:
time: 53.9 us; the launch traced here: 53.7 us
  Pallas kernels  51.6 us (96%)
  local copies, waits for them, and re-layouts  1.43 us (3%)
  between operations  0.64 us (1%)
    pallas_call x1, Pallas kernels, body(): pl.pallas_call(kernel, out_shape=jax.ShapeDtypeStruct((3, B, B), BF16), i...  51.6 us
    squeeze x1, local copies, waits for them, and re-layouts, body(): return (grads[0], grads[1], grads[2])  1.43 us

profile of v4, /device:TPU:1, one launch (start us, length us, event | category | flops | bytes accessed | tf_op | source)
XLA Modules:
  0.0 53.7 jit_solution(13283575153445802248)
XLA Ops:
  0.6 51.6 %attention_backward.1 = bf16[3,128,128]{2,1,0:T(8,128)(2,1)} custom-call(bf16[128,128]{1,0:T(8,128)(2,1)} %q_ref.1, bf16[128,128]{1,0:T(8,128)(2,1)} %k_ref.1, bf16[128,128]{1,0:T(8,128)(2,1)} %v_ref.1, bf16[128,128]{1,0:T(8,128)(2,1)} %g_ref.1, s32[256,128]{1,0:T(8,128)} %bitcast.7), custom_call_target="tpu_custom_call" | custom-call | tf_op jit(solution)/shard_map/attention_backward/pallas_call | solution.py:404
  52.3 1.4 %slice_bitcast_fusion = (bf16[128,128]{1,0:T(8,128)(2,1)}, bf16[128,128]{1,0:T(8,128)(2,1)}, bf16[128,128]{1,0:T(8,128)(2,1)}) fusion(bf16[3,128,128]{2,1,0:T(8,128)(2,1)} %attention_backward.1), kind=kLoop, calls=%fused_computation | loop fusion | bytes 196608 | tf_op jit(solution)/shard_map/squeeze | solution.py:448

commit v5 on v4

--- a/solution.py
+++ b/solution.py
@@ -31,7 +31,7 @@
 def kernel(
     q_ref, k_ref, v_ref, g_ref, pos_hbm, out_ref,
     qb, gb, kvb, pos_ref, ktb, posk, posq, s_buf, dp_buf, mt, zt, dt, stat_out, stat_in, factor, tops,
-    w_buf, e_buf, q_scaled, g_scaled, part, tmp, pair_out, pair_in, z_out, z_in, q_out, q_in,
+    w_buf, e_buf, sums, q_scaled, g_scaled, part, tmp, pair_out, pair_in, z_out, z_in, q_out, q_in,
     ins, gs, gr, ss, sr, ps, pr, zs, zr, qs_sem, qr_sem,
 ):
     row, col = lax.axis_index("row"), lax.axis_index("col")
@@ -239,15 +239,18 @@
 
     def weigh(t, carry):
         top, mean = tops[t, 0:1, :], tops[t, 1:2, :]
-
-        def step(i, carry):
-            for zz in (2 * i, 2 * i + 1):
+        of_e = of_w = None
+        for zz in range(9):
+            if zz < 8:
                 w = jnp.exp2(s_buf[t, zz] - top)
                 w_buf[t, zz] = w.astype(BF16)
                 e_buf[t, zz] = (w * (dp_buf[t, zz] - mean)).astype(BF16)
-            return carry
-
-        return lax.fori_loop(0, 4, step, carry)
+            if zz:
+                by_e, by_w = (nn(ktb[zz - 1], buf[t, zz - 1]) for buf in (e_buf, w_buf))
+                of_e, of_w = (by_e, by_w) if zz == 1 else (of_e + by_e, of_w + by_w)
+        sums[t, 0] = of_e
+        sums[t, 1] = of_w
+        return carry
 
     lax.fori_loop(0, 4, weigh, 0)
 
@@ -280,16 +283,11 @@
 
     def query_side(i):
         t = column(i)
-        of_e = nn(ktb[0], e_buf[t, 0])
-        of_w = nn(ktb[0], w_buf[t, 0])
-        for zz in range(1, 8):
-            of_e += nn(ktb[zz], e_buf[t, zz])
-            of_w += nn(ktb[zz], w_buf[t, zz])
         for j in range(4):
             here = slice(j * B, (j + 1) * B)
             f = factor[0, pl.ds(4 * t + j, 1), :]
             h = factor[1, pl.ds(4 * t + j, 1), :]
-            q_out[4 * i + j] = (of_e[:, here] * f + of_w[:, here] * h).astype(BF16)
+            q_out[4 * i + j] = (sums[t, 0, :, here] * f + sums[t, 1, :, here] * h).astype(BF16)
         for j in (2, 1, 3, 0):
             if (i, j) != (3, 0):
                 q_copy(i, j).start()
@@ -354,24 +352,24 @@
         pair_copy(off).start()
 
     key_side(4)
+    query_side(0)
     key_side(3)
+    query_side(1)
     key_side(5)
-    key_side(2)
-    pass_on(4)
-    key_side(6)
-    pass_on(3)
-    query_side(0)
-    pass_on(5)
-    query_side(1)
     query_side(2)
     query_side(3)
     key_side(1)
+    pass_on(4)
     key_side(7)
+    pass_on(3)
+    key_side(2)
+    pass_on(5)
+    pass_on(1)
+    key_side(6)
+    pass_on(7)
     key_side(0)
     pass_on(2)
     pass_on(6)
-    pass_on(1)
-    pass_on(7)
 
     scale = 1.0 / math.sqrt(B)
     pair_copy(0).wait_recv()
@@ -424,6 +422,7 @@
             pltpu.VMEM((4, 8, 4 * B), F32),
             pltpu.VMEM((4, 8, 2 * B, 4 * B), BF16),
             pltpu.VMEM((4, 8, 2 * B, 4 * B), BF16),
+            pltpu.VMEM((4, 2, B, 4 * B), F32),
             pltpu.VMEM((16, B, B), BF16),
             pltpu.VMEM((16, B, 2 * B), BF16),
             pltpu.VMEM((8, 2, B, B), F32),

time: 53.9 us -> 50.4 us (0.935)
  the two profiles are of different devices: /device:TPU:1 before, /device:TPU:2 now
where the time goes in v5:
time: 50.4 us; the launch traced here: 50.2 us
  Pallas kernels  48.2 us (96%)
  local copies, waits for them, and re-layouts  1.43 us (3%)
  between operations  0.64 us (1%)
    pallas_call x1, Pallas kernels, body(): pl.pallas_call(kernel, out_shape=jax.ShapeDtypeStruct((3, B, B), BF16), i...  48.2 us
    squeeze x1, local copies, waits for them, and re-layouts, body(): return (grads[0], grads[1], grads[2])  1.43 us

profile of v5, /device:TPU:2, one launch (start us, length us, event | category | flops | bytes accessed | tf_op | source)
XLA Modules:
  0.0 50.2 jit_solution(10460847106093419842)
XLA Ops:
  0.6 48.2 %attention_backward.1 = bf16[3,128,128]{2,1,0:T(8,128)(2,1)} custom-call(bf16[128,128]{1,0:T(8,128)(2,1)} %q_ref.1, bf16[128,128]{1,0:T(8,128)(2,1)} %k_ref.1, bf16[128,128]{1,0:T(8,128)(2,1)} %v_ref.1, bf16[128,128]{1,0:T(8,128)(2,1)} %g_ref.1, s32[256,128]{1,0:T(8,128)} %bitcast.7), custom_call_target="tpu_custom_call" | custom-call | tf_op jit(solution)/shard_map/attention_backward/pallas_call | solution.py:402
  48.8 1.4 %slice_bitcast_fusion = (bf16[128,128]{1,0:T(8,128)(2,1)}, bf16[128,128]{1,0:T(8,128)(2,1)}, bf16[128,128]{1,0:T(8,128)(2,1)}) fusion(bf16[3,128,128]{2,1,0:T(8,128)(2,1)} %attention_backward.1), kind=kLoop, calls=%fused_computation | loop fusion | bytes 196608 | tf_op jit(solution)/shard_map/squeeze | solution.py:447

commit v6 on v5

--- a/solution.py
+++ b/solution.py
@@ -340,11 +340,9 @@
 
     def key_side(off):
         zz = up8(z, off)
-        dk = jnp.zeros((2 * B, B), F32)
-        dvk = jnp.zeros((2 * B, 2 * B), F32)
-        for t in range(4):
-            dk += nn(e_buf[t, zz], q_scaled[4 * t : 4 * t + 4].reshape(4 * B, B))
-            dvk += nn(w_buf[t, zz], g_scaled[4 * t : 4 * t + 4].reshape(4 * B, 2 * B))
+        e_row, w_row = (jnp.concatenate([buf[t, zz] for t in range(4)], axis=1) for buf in (e_buf, w_buf))
+        dk = nn(e_row, q_scaled[...].reshape(16 * B, B))
+        dvk = nn(w_row, g_scaled[...].reshape(16 * B, 2 * B))
         for w, total in enumerate((dk + dvk[:, B:], dvk[:, :B])):
             tmp[w] = total.reshape(2, B, B)
             part[off, w] = tmp[w, c]
@@ -352,18 +350,18 @@
         pair_copy(off).start()
 
     key_side(4)
+    key_side(3)
     query_side(0)
-    key_side(3)
+    key_side(5)
+    pass_on(4)
     query_side(1)
-    key_side(5)
     query_side(2)
     query_side(3)
     key_side(1)
-    pass_on(4)
+    pass_on(3)
     key_side(7)
-    pass_on(3)
+    pass_on(5)
     key_side(2)
-    pass_on(5)
     pass_on(1)
     key_side(6)
     pass_on(7)

time: 50.4 us -> 49.7 us (0.986)
  the two profiles are of different devices: /device:TPU:2 before, /device:TPU:1 now
where the time goes in v6:
time: 49.7 us; the launch traced here: 49.5 us
  Pallas kernels  47.5 us (96%)
  local copies, waits for them, and re-layouts  1.43 us (3%)
  between operations  0.64 us (1%)
    pallas_call x1, Pallas kernels, body(): pl.pallas_call(kernel, out_shape=jax.ShapeDtypeStruct((3, B, B), BF16), i...  47.5 us
    squeeze x1, local copies, waits for them, and re-layouts, body(): return (grads[0], grads[1], grads[2])  1.43 us

profile of v6, /device:TPU:1, one launch (start us, length us, event | category | flops | bytes accessed | tf_op | source)
XLA Modules:
  0.0 49.5 jit_solution(107442550827081761)
XLA Ops:
  0.6 47.5 %attention_backward.1 = bf16[3,128,128]{2,1,0:T(8,128)(2,1)} custom-call(bf16[128,128]{1,0:T(8,128)(2,1)} %q_ref.1, bf16[128,128]{1,0:T(8,128)(2,1)} %k_ref.1, bf16[128,128]{1,0:T(8,128)(2,1)} %v_ref.1, bf16[128,128]{1,0:T(8,128)(2,1)} %g_ref.1, s32[256,128]{1,0:T(8,128)} %bitcast.7), custom_call_target="tpu_custom_call" | custom-call | tf_op jit(solution)/shard_map/attention_backward/pallas_call | solution.py:400
  48.1 1.4 %slice_bitcast_fusion = (bf16[128,128]{1,0:T(8,128)(2,1)}, bf16[128,128]{1,0:T(8,128)(2,1)}, bf16[128,128]{1,0:T(8,128)(2,1)}) fusion(bf16[3,128,128]{2,1,0:T(8,128)(2,1)} %attention_backward.1), kind=kLoop, calls=%fused_computation | loop fusion | bytes 196608 | tf_op jit(solution)/shard_map/squeeze | solution.py:445
